TPU v7x, 32 devices: a whole 2x2x4 slice. The times are simulated.
32 devices in a mesh: gx: 4 (over x, core), gy: 4 (over z), gz: 2 (over y).
Axes of the slice: x: 2, y: 2, z: 4, core: 2. Of those that a mesh axis runs over, the one named last changes fastest.
Arguments:
- columns: int32 [1024, 2048], P(('gx', 'gy', 'gz')), may hold values from 0 to 32767, as said below
- counts: int32 [1024, 2048], P(('gx', 'gy', 'gz')), may hold values from 1 to 63
- nnz_count: int32 [1024], P(('gx', 'gy', 'gz')), may hold values from 1 to 2048, as said below
- selected: int32 [2048], replicated, may hold values from 0 to 32767, as said below
Outputs:
- gene_stats: float32 [2, 32768], P(None, 'gz')
- pca_input: bfloat16 [1024, 2048], P(('gx', 'gy'), 'gz')
Inputs may be any that keep to these rules, and one draw needn't show every extreme that they name: `columns`: in each row no two slots fall in the same block of 16 consecutive genes (so the first nnz_count slots hold distinct genes); slots beyond nnz_count are not part of the matrix. For every k, the live slots of one cell fall on at most 128 of the genes selected[k * 2048 / 2] to selected[(k + 1) * 2048 / 2 - 1]; some cell reaches 128 for every k in every draw. `nnz_count`: some cell has all 2048 slots live in every draw. `selected`: distinct genes.
All inputs are finite; a program needn't handle non-finite values.
Results may differ from a plain program's by a relative error of at most 0.0085.
Values may be sent and summed in bfloat16 or wider, within the bound.
A program may use at most 128 MiB of HBM per device.

v0:
```python
import functools

import jax
import jax.numpy as jnp
from jax import lax
from jax.experimental import pallas as pl
from jax.experimental.pallas import tpu as pltpu
from jax.sharding import PartitionSpec as P

GENES = 32768
BLOCK = 16
LANES = 128

target_sum = 10000.0
var_floor = 0.01
clip_value = 10.0

MESH = pl.DeviceIdType.MESH


def fused_kernel(
    sizes, cells, columns_ref, counts_ref, nnz_ref, selected_ref, stats_ref, sel_stats_ref, moved_ref,
    value_rows, high_rows, low_rows, offset_rows, block_values, block_offsets, table,
    sums_ref, sel_sums_ref, dense_ref, got, sel_got, mine, sel_mine, send_sem, recv_sem,
):
    nx, ny, owners = sizes
    teams = nx * ny
    n = teams * owners
    gx, gy, z = lax.axis_index("gx"), lax.axis_index("gy"), lax.axis_index("gz")
    r = gx * ny + gy
    me = r * owners + z

    def place(team, owner):
        return {"gx": lax.div(team, ny), "gy": lax.rem(team, ny), "gz": owner}

    def split(k):
        other = lax.rem(me + k, n)
        return other, place(lax.div(other, owners), lax.rem(other, owners))

    barrier = pltpu.get_barrier_semaphore()

    def greet(k, carry):
        pl.semaphore_signal(barrier, inc=1, device_id=split(k)[1], device_id_type=MESH)
        return carry

    lax.fori_loop(1, n, greet, 0)

    def send(src, dst, kind, where):
        pltpu.make_async_remote_copy(
            src_ref=src, dst_ref=dst, send_sem=send_sem.at[kind], recv_sem=recv_sem.at[kind],
            device_id=where, device_id_type=MESH,
        ).start()

    def finish(sem, ref, count):
        span = ref.at[pl.ds(0, count)]
        pltpu.make_async_copy(span, span, sem).wait()

    local, slots = columns_ref.shape
    high_count = GENES // (BLOCK * LANES)
    rows = high_count // owners
    bf16, f32 = jnp.bfloat16, jnp.float32

    sub = lax.broadcasted_iota(jnp.int32, (local, local), 0)
    lane = lax.broadcasted_iota(jnp.int32, (local, local), 1)
    live_count = jnp.sum(jnp.where(sub == lane, nnz_ref[...], 0), axis=1, keepdims=True)
    slot = lax.broadcasted_iota(jnp.int32, (local, slots), 1)
    live = slot < live_count
    raw = jnp.where(live, counts_ref[...].astype(f32), 0.0)
    library = jnp.sum(raw, axis=1, keepdims=True)
    value_rows[...] = jnp.log1p(raw * (target_sum / library))
    genes = columns_ref[...]
    upper = (lax.shift_right_logical(genes, 10) & 1) * high_count
    high_rows[...] = (lax.shift_right_logical(genes, 11) + upper).astype(f32)
    low_rows[...] = (lax.shift_right_logical(genes, 4) & (LANES // 2 - 1)).astype(f32)
    offset_rows[...] = jnp.where(live, genes & (BLOCK - 1), 0).astype(f32)

    ids = lax.broadcasted_iota(jnp.int32, (16, slots), 0).astype(f32).astype(bf16)

    def spread(ref, c):
        return jnp.broadcast_to(ref[pl.ds(c, 1), :], (16, slots)).astype(bf16)

    def one_cell(c, carry):
        zero, one = bf16(0.0), bf16(1.0)
        high = spread(high_rows, c)
        hits = [high == ids + bf16(high_count * k) for k in range(2)]
        value, offset = spread(value_rows, c), spread(offset_rows, c)
        left = jnp.concatenate(
            [jnp.where(hit, line, zero) for line in (value, offset) for hit in hits], axis=0
        )
        low = spread(low_rows, c)
        right = jnp.concatenate(
            [jnp.where(low == ids + bf16(16 * k), one, zero) for k in range(LANES // 32)], axis=0
        )
        placed = lax.dot_general(left, right, (((1,), (1,)), ((), ())), preferred_element_type=f32)
        quarters = [placed[high_count * k:high_count * (k + 1)] for k in range(4)]
        block_values[c] = jnp.concatenate(quarters[:2], axis=1)
        block_offsets[c] = jnp.concatenate(quarters[2:], axis=1)
        return carry

    lax.fori_loop(0, local, one_cell, 0, unroll=8)

    for half in range(high_count // 8):
        span = slice(8 * half, 8 * half + 8)

        def add_cell(c, carry):
            v = block_values[c, span, :]
            o = block_offsets[c, span, :]
            w = v * v
            out = []
            for k in range(BLOCK):
                hit = o == float(k)
                out.append(carry[2 * k] + jnp.where(hit, v, 0.0))
                out.append(carry[2 * k + 1] + jnp.where(hit, w, 0.0))
            return tuple(out)

        parts = lax.fori_loop(0, local, add_cell, (jnp.zeros((8, LANES), f32),) * (2 * BLOCK), unroll=4)
        for k in range(BLOCK):
            near = parts[2 * k] * (1.0 / local)
            spare = parts[2 * k + 1] - parts[2 * k] * near
            step = min(rows, 8)
            for first in range(0, 8, step):
                owner = (8 * half + first) // rows
                pair = jnp.concatenate([near[first:first + step], spare[first:first + step]], axis=0)
                sums_ref[k * owners + owner] = pair.astype(bf16)

    for high in range(high_count):
        cols = slice(high * LANES, (high + 1) * LANES)
        table[0:local, cols] = block_values[:, high, :].astype(bf16)
        table[local:, cols] = block_offsets[:, high, :].astype(bf16)

    pl.semaphore_wait(barrier, n - 1)

    def scatter(k, carry):
        other, where = split(k)
        send(sums_ref.at[other], got.at[me], 0, where)
        return carry

    lax.fori_loop(1, n, scatter, 0)
    got[me] = sums_ref[me]

    share = dense_ref.shape[2]
    tiles = share // LANES
    chunk = min(256, share)
    blocks = GENES // BLOCK
    sel_sums_ref[...] = jnp.zeros_like(sel_sums_ref)
    chunk_ids = lax.broadcasted_iota(jnp.int32, (16, chunk), 0).astype(f32).astype(bf16)
    for first in range(0, owners * share, chunk):
        picked = selected_ref[:, first:first + chunk]
        block = lax.shift_right_logical(picked, 4)
        pieces = []
        for group in range(blocks // 256):
            inside = jnp.where(lax.shift_right_logical(block, 8) == group, block & 255, -1).astype(f32)
            inside = jnp.broadcast_to(inside, (16, chunk)).astype(bf16)
            for k in range(16):
                pieces.append(jnp.where(inside == chunk_ids + bf16(16 * k), bf16(1.0), bf16(0.0)))
        found = jnp.dot(table[...], jnp.concatenate(pieces, axis=0), preferred_element_type=f32)
        wanted = (picked & (BLOCK - 1)).astype(f32)
        x = jnp.where(found[local:] == wanted, found[:local], 0.0)
        owner, start = first // share, first % share
        dense_ref[owner, :, start:start + chunk] = x.astype(bf16)
        total = jnp.sum(x, axis=0, keepdims=True)
        square = jnp.sum(x * x, axis=0, keepdims=True)
        for stat, line in enumerate((total, square)):
            for tile in range(chunk // LANES):
                line_row = stat * tiles + start // LANES + tile
                sel_sums_ref[line_row * owners + owner] = line[:, tile * LANES:(tile + 1) * LANES]

    def move(k, carry):
        owner = lax.rem(z + k, owners)
        send(dense_ref.at[owner], moved_ref.at[z], 2, place(r, owner))
        return carry

    def sel_scatter(k, carry):
        other, where = split(k)
        send(sel_sums_ref.at[other], sel_got.at[me], 1, where)
        return carry

    lax.fori_loop(1, n, sel_scatter, 0)
    lax.fori_loop(1, owners, move, 0)
    sel_got[me] = sel_sums_ref[me]
    moved_ref[z] = dense_ref[z]

    finish(recv_sem.at[0], got, n - 1)
    parts = got[...].astype(f32)
    means = parts[:, :rows]
    mean = jnp.sum(means, axis=0) * (1.0 / n)
    away = means - mean[None]
    variance = jnp.sum(parts[:, rows:] + (away * away) * float(local), axis=0) * (1.0 / cells)
    mine[...] = jnp.concatenate([mean, variance], axis=0).astype(bf16)

    def gather(k, carry):
        send(mine, stats_ref.at[r], 3, place(lax.rem(r + k, teams), z))
        return carry

    def sel_gather(k, carry):
        send(sel_mine, sel_stats_ref.at[r], 4, place(lax.rem(r + k, teams), z))
        return carry

    lax.fori_loop(1, teams, gather, 0)
    finish(recv_sem.at[1], sel_got, n - 1)
    sel_mine[...] = jnp.sum(sel_got[...], axis=0)
    stats_ref[r] = mine[...]
    lax.fori_loop(1, teams, sel_gather, 0)
    sel_stats_ref[r] = sel_mine[...]
    finish(recv_sem.at[2], moved_ref, owners - 1)
    finish(send_sem.at[0], got, n - 1)
    finish(send_sem.at[1], sel_got, n - 1)
    finish(send_sem.at[2], moved_ref, owners - 1)
    finish(recv_sem.at[3], stats_ref, teams - 1)
    finish(recv_sem.at[4], sel_stats_ref, teams - 1)
    finish(send_sem.at[3], stats_ref, teams - 1)
    finish(send_sem.at[4], sel_stats_ref, teams - 1)


def final_kernel(cells, stats_ref, sel_stats_ref, moved_ref, gene_ref, pca_ref, turned):
    teams, double, lanes = stats_ref.shape
    rows = double // 2
    stats = stats_ref[...].astype(jnp.float32)
    for stat in range(2):
        for row in range(rows):
            turned[row * lanes:(row + 1) * lanes, :] = jnp.transpose(stats[:, stat * rows + row, :])
        lines = rows * lanes // 8
        parts = [turned[pl.ds(k, lines, stride=8), :] for k in range(8)]
        gene_ref[:, stat, :] = jnp.concatenate(parts, axis=1)
    owners, local, share = moved_ref.shape
    tiles = share // lanes
    for tile in range(tiles):
        mean = sel_stats_ref[tile] * (1.0 / cells)
        variance = sel_stats_ref[tiles + tile] * (1.0 / cells) - mean * mean
        scale = jnp.sqrt(jnp.maximum(variance, var_floor))
        cols = slice(tile * lanes, (tile + 1) * lanes)
        for owner in range(owners):
            x = moved_ref[owner, :, cols].astype(jnp.float32)
            y = jnp.clip((x - mean) / scale, -clip_value, clip_value)
            pca_ref[owner * local:(owner + 1) * local, cols] = y.astype(jnp.bfloat16)


def per_device(sizes, columns, counts, nnz_count, selected):
    f32, bf16 = jnp.float32, jnp.bfloat16
    nx, ny, owners = sizes
    teams = nx * ny
    n = teams * owners
    local, slots = columns.shape
    cells = local * n
    high_count = GENES // (BLOCK * LANES)
    rows = high_count // owners
    share = selected.shape[0] // owners
    assert teams == BLOCK and rows * owners == high_count and rows <= 8 and 2 * share // LANES <= teams
    vmem = pl.BlockSpec(memory_space=pltpu.VMEM)
    stats, sel_stats, moved = pl.pallas_call(
        functools.partial(fused_kernel, sizes, cells),
        name="sums_and_exchange",
        out_shape=(
            jax.ShapeDtypeStruct((teams, 2 * rows, LANES), bf16),
            jax.ShapeDtypeStruct((teams, 1, LANES), f32),
            jax.ShapeDtypeStruct((owners, local, share), bf16),
        ),
        in_specs=[vmem] * 4,
        out_specs=(vmem,) * 3,
        scratch_shapes=[pltpu.VMEM((local, slots), f32)] * 4
        + [pltpu.VMEM((local, high_count, LANES), f32)] * 2
        + [pltpu.VMEM((2 * local, GENES // BLOCK), bf16)]
        + [
            pltpu.VMEM((n, 2 * rows, LANES), bf16),
            pltpu.VMEM((n, 1, LANES), f32),
            pltpu.VMEM((owners, local, share), bf16),
            pltpu.VMEM((n, 2 * rows, LANES), bf16),
            pltpu.VMEM((n, 1, LANES), f32),
            pltpu.VMEM((2 * rows, LANES), bf16),
            pltpu.VMEM((1, LANES), f32),
            pltpu.SemaphoreType.DMA((5,)),
            pltpu.SemaphoreType.DMA((5,)),
        ],
        compiler_params=pltpu.CompilerParams(collective_id=0, has_side_effects=True),
    )(columns, counts, nnz_count.reshape(1, local), selected.reshape(1, -1))
    lines = GENES // owners // LANES
    gene_stats, pca_input = pl.pallas_call(
        functools.partial(final_kernel, cells),
        name="standardize",
        out_shape=(
            jax.ShapeDtypeStruct((lines, 2, LANES), f32),
            jax.ShapeDtypeStruct((owners * local, share), bf16),
        ),
        in_specs=[vmem] * 3,
        out_specs=(vmem,) * 2,
        scratch_shapes=[pltpu.VMEM((rows * LANES, teams), f32)],
    )(stats, sel_stats, moved)
    return (gene_stats.transpose(1, 0, 2).reshape(2, -1), pca_input)


def solution(mesh):
    sizes = tuple(mesh.shape[axis] for axis in ("gx", "gy", "gz"))
    return jax.shard_map(
        functools.partial(per_device, sizes),
        mesh=mesh,
        in_specs=(
            P(("gx", "gy", "gz"), None),
            P(("gx", "gy", "gz"), None),
            P(("gx", "gy", "gz")),
            P(),
        ),
        out_specs=(P(None, "gz"), P(("gx", "gy"), "gz")),
        check_vma=False,
    )
```

profile of v0, /device:TPU:0, one launch (start us, length us, event | category | flops | bytes accessed | tf_op | source)
XLA Modules:
  0.0 23.4 jit_solution(5211135256692373382)
XLA Ops:
  0.6 20.6 %sums_and_exchange.1 = (bf16[16,16,128]{2,1,0:T(8,128)(2,1)}, f32[16,1,128]{2,1,0:T(1,128)}, bf16[2,32,1024]{2,1,0:T(8,128)(2,1)}) custom-call(s32[32,2048]{1,0:T(8,128)} %columns_ref.1, s32[32,2048]{1,0:T(8,128)} %counts_ref.1, s32[1,32]{1,0:T(1,128)} %bitcast.6, s32[1,2048]{1,0:T(1,128)} %bitcast.5), custom_call_target="tpu_custom_call" | custom-call | tf_op jit(solution)/shard_map/sums_and_exchange/pallas_call | solution.py:250
  21.2 2.2 %standardize.1 = (f32[128,2,128]{2,1,0:T(2,128)}, bf16[64,1024]{1,0:T(8,128)(2,1)}) custom-call(bf16[16,16,128]{2,1,0:T(8,128)(2,1)} %get-tuple-element.7.stats_ref, f32[16,1,128]{2,1,0:T(1,128)} %get-tuple-element.8.sel_stats_ref, bf16[2,32,1024]{2,1,0:T(8,128)(2,1)} %get-tuple-element.9.moved_ref), custom_call_target="tpu_custom_call" | custom-call | tf_op jit(solution)/shard_map/standardize/pallas_call | solution.py:277
where the time goes:
time: 23.6 us; the launch traced here: 23.4 us
  Pallas kernels  22.8 us (97%)
  between operations  0.64 us (3%)
    pallas_call x1, Pallas kernels, per_device(): pl.pallas_call(functools.partial(fused_kernel, sizes, cells), name='sums_...  20.6 us
    pallas_call x1, Pallas kernels, per_device(): pl.pallas_call(functools.partial(final_kernel, cells), name='standardize'...  2.2 us

commit v1 on v0

v1 whole, which is shorter than its diff:
```python
import functools

import jax
import jax.numpy as jnp
from jax import lax
from jax.experimental import pallas as pl
from jax.experimental.pallas import tpu as pltpu
from jax.sharding import PartitionSpec as P

GENES = 32768
BLOCK = 16
LANES = 128
GROUP = 8
HIGHS = GENES // (BLOCK * LANES)

target_sum = 10000.0
var_floor = 0.01
clip_value = 10.0

MESH = pl.DeviceIdType.MESH


def flip(value, k, size):
    out, bit = 0, 1
    while bit < size:
        part = lax.rem(lax.div(value, bit), 2)
        out = out + (1 - part if k & bit else part) * bit
        bit *= 2
    return out


def fused_kernel(
    sizes, cells, columns_hbm, counts_hbm, nnz_hbm, selected_hbm, gene_ref, pca_ref,
    columns_ref, counts_ref, nnz_ref, selected_ref, value_rows, high_rows, low_rows, offset_rows,
    near_values, near_squares, near_offsets, far_values, far_offsets, acc_values, acc_squares, table,
    sums_ref, sel_sums_ref, dense_ref, got, sel_got, mine, sel_mine, stats_ref, sel_stats_ref, moved_ref,
    wide, turned, load_sem, send_sem, recv_sem,
):
    nx, ny, owners = sizes
    teams = nx * ny
    n = teams * owners
    gx, gy, z = lax.axis_index("gx"), lax.axis_index("gy"), lax.axis_index("gz")
    r = gx * ny + gy
    me = r * owners + z
    bf16, f32 = jnp.bfloat16, jnp.float32
    local, slots = columns_ref.shape
    groups = local // GROUP
    tiles = slots // LANES
    rows = HIGHS // owners

    loads = [pltpu.make_async_copy(nnz_hbm, nnz_ref, load_sem.at[0])]
    for g in range(groups):
        span = pl.ds(g * GROUP, GROUP)
        loads.append(pltpu.make_async_copy(counts_hbm.at[span], counts_ref.at[span], load_sem.at[1 + 2 * g]))
        loads.append(pltpu.make_async_copy(columns_hbm.at[span], columns_ref.at[span], load_sem.at[2 + 2 * g]))
    loads.append(pltpu.make_async_copy(selected_hbm, selected_ref, load_sem.at[1 + 2 * groups]))
    for load in loads:
        load.start()

    small = n <= 64
    if small:
        xs = [flip(gx, k, nx) for k in range(nx)]
        ys = [flip(gy, k, ny) for k in range(ny)]
        zs = [flip(z, k, owners) for k in range(owners)]
        steps = [(kx, ky, kz) for ky in range(ny) for kx in range(nx) for kz in range(owners)]
        steps = [step for step in reversed(steps) if any(step)]

    def each_device(act):
        if small:
            for kx, ky, kz in steps:
                other = (xs[kx] * ny + ys[ky]) * owners + zs[kz]
                act(other, {"gx": xs[kx], "gy": ys[ky], "gz": zs[kz]})
            return

        def step(k, carry):
            other = lax.rem(me + k, n)
            team, owner = lax.div(other, owners), lax.rem(other, owners)
            act(other, {"gx": lax.div(team, ny), "gy": lax.rem(team, ny), "gz": owner})
            return carry

        lax.fori_loop(1, n, step, 0)

    def each_team(act):
        if small:
            for kx, ky, kz in steps:
                if kz == 0:
                    act({"gx": xs[kx], "gy": ys[ky], "gz": z})
            return

        def step(k, carry):
            team = lax.rem(r + k, teams)
            act({"gx": lax.div(team, ny), "gy": lax.rem(team, ny), "gz": z})
            return carry

        lax.fori_loop(1, teams, step, 0)

    barrier = pltpu.get_barrier_semaphore()
    each_device(
        lambda other, where: pl.semaphore_signal(barrier, inc=1, device_id=where, device_id_type=MESH)
    )

    def send(src, dst, kind, where):
        pltpu.make_async_remote_copy(
            src_ref=src, dst_ref=dst, send_sem=send_sem.at[kind], recv_sem=recv_sem.at[kind],
            device_id=where, device_id_type=MESH,
        ).start()

    def finish(sem, ref, count):
        span = ref.at[pl.ds(0, count)]
        pltpu.make_async_copy(span, span, sem).wait()

    ids = lax.broadcasted_iota(jnp.int32, (16, slots), 0).astype(f32).astype(bf16)
    sub = lax.broadcasted_iota(jnp.int32, (GROUP, local), 0)
    lane = lax.broadcasted_iota(jnp.int32, (GROUP, local), 1)
    slot = lax.broadcasted_iota(jnp.int32, (GROUP, slots), 1)

    def prepare(g):
        loads[1 + 2 * g].wait()
        span = slice(g * GROUP, (g + 1) * GROUP)
        live_count = jnp.sum(jnp.where(sub + g * GROUP == lane, nnz_ref[...], 0), axis=1, keepdims=True)
        live = slot < live_count
        raw = jnp.where(live, counts_ref[span, :].astype(f32), 0.0)
        library = jnp.sum(raw, axis=1, keepdims=True)
        value = jnp.log(1.0 + raw * (target_sum / library))
        loads[2 + 2 * g].wait()
        genes = columns_ref[span, :]
        upper = (lax.shift_right_logical(genes, 10) & 1) * HIGHS
        high = (lax.shift_right_logical(genes, 11) + upper).astype(f32)
        low = (lax.shift_right_logical(genes, 4) & (LANES // 2 - 1)).astype(f32)
        offset = jnp.where(live, genes & (BLOCK - 1), 0).astype(f32)
        for tile in range(tiles):
            at = (g * tiles + tile) * GROUP
            cols = slice(tile * LANES, (tile + 1) * LANES)
            for ref, line in ((value_rows, value), (high_rows, high), (low_rows, low), (offset_rows, offset)):
                ref[at:at + GROUP, :] = line[:, cols]

    def spread(ref, g, j):
        return jnp.concatenate(
            [ref[pl.ds((g * tiles + tile) * GROUP + j, 16, stride=0), :].astype(bf16) for tile in range(tiles)],
            axis=1,
        )

    def place(g, j):
        c = g * GROUP + j
        zero, one = bf16(0.0), bf16(1.0)
        high = spread(high_rows, g, j)
        hits = [high == ids + bf16(HIGHS * k) for k in range(2)]
        value, offset = spread(value_rows, g, j), spread(offset_rows, g, j)
        left = jnp.concatenate(
            [jnp.where(hit, line, zero) for line in (value, offset) for hit in hits], axis=0
        )
        low = spread(low_rows, g, j)
        right = jnp.concatenate(
            [jnp.where(low == ids + bf16(16 * k), one, zero) for k in range(LANES // 32)], axis=0
        )
        placed = lax.dot_general(left, right, (((1,), (1,)), ((), ())), preferred_element_type=f32)
        quarters = [placed[HIGHS * k:HIGHS * (k + 1)] for k in range(4)]
        v = jnp.concatenate(quarters[:2], axis=1)
        o = jnp.concatenate(quarters[2:], axis=1)
        near_values[c], near_squares[c], near_offsets[c] = v, v * v, o
        far_values[pl.ds(c, HIGHS, stride=local), :] = v
        far_offsets[pl.ds(c, HIGHS, stride=local), :] = o

    def gather_sums(g, ks):
        total = [jnp.zeros((HIGHS, LANES), f32) if g == 0 else acc_values[k] for k in ks]
        square = [jnp.zeros((HIGHS, LANES), f32) if g == 0 else acc_squares[k] for k in ks]
        for j in range(GROUP):
            c = g * GROUP + j
            v, w, o = near_values[c], near_squares[c], near_offsets[c]
            for i, k in enumerate(ks):
                hit = o == float(k)
                total[i] = total[i] + jnp.where(hit, v, 0.0)
                square[i] = square[i] + jnp.where(hit, w, 0.0)
        for i, k in enumerate(ks):
            if g < groups - 1:
                acc_values[k], acc_squares[k] = total[i], square[i]
                continue
            near = total[i] * (1.0 / local)
            spare = square[i] - total[i] * near
            for owner in range(owners):
                part = slice(owner * rows, (owner + 1) * rows)
                sums_ref[k * owners + owner] = jnp.concatenate([near[part], spare[part]], axis=0).astype(bf16)

    per_cell = BLOCK // GROUP
    loads[0].wait()
    for g in range(groups):
        with jax.named_scope("prep"):
            prepare(g)
        with jax.named_scope("place"):
            for j in range(GROUP):
                place(g, j)
                if g:
                    gather_sums(g - 1, range(j * per_cell, (j + 1) * per_cell))
    with jax.named_scope("tail"):
        for j in range(GROUP):
            gather_sums(groups - 1, range(j * per_cell, (j + 1) * per_cell))

    with jax.named_scope("barrier_wait"):
        pl.semaphore_wait(barrier, n - 1)
    with jax.named_scope("scatter_send"):
        each_device(lambda other, where: send(sums_ref.at[other], got.at[me], 0, where))
    got[me] = sums_ref[me]

    with jax.named_scope("select"):
        share = dense_ref.shape[2]
        out_tiles = share // LANES
        chunk = min(256, share)
        pairs = HIGHS // 2
        for pair in range(pairs):
            for part, ref in enumerate((far_values, far_offsets)):
                at = 2 * pair * local
                line = jnp.concatenate([ref[at:at + local, :], ref[at + local:at + 2 * local, :]], axis=1)
                at = (2 * pair + part) * local
                table[at:at + local, :] = line.astype(bf16)
        sel_sums_ref[...] = jnp.zeros_like(sel_sums_ref)
        chunk_ids = lax.broadcasted_iota(jnp.int32, (16, chunk), 0).astype(f32).astype(bf16)
        loads[1 + 2 * groups].wait()
        for first in range(0, owners * share, chunk):
            picked = selected_ref[:, first:first + chunk]
            inside = (lax.shift_right_logical(picked, 4) & (2 * LANES - 1)).astype(f32)
            inside = jnp.broadcast_to(inside, (16, chunk)).astype(bf16)
            one_hot = jnp.concatenate(
                [jnp.where(inside == chunk_ids + bf16(16 * k), bf16(1.0), bf16(0.0)) for k in range(16)], axis=0
            )
            found = jnp.dot(table[...], one_hot, preferred_element_type=f32)
            which = jnp.broadcast_to(lax.shift_right_logical(picked, 12), (2 * local, chunk))
            mix = found[:2 * local]
            for pair in range(1, pairs):
                mix = jnp.where(which == pair, found[2 * local * pair:2 * local * (pair + 1)], mix)
            wanted = (picked & (BLOCK - 1)).astype(f32)
            x = jnp.where(mix[local:] == wanted, mix[:local], 0.0)
            owner, start = first // share, first % share
            dense_ref[owner, :, start:start + chunk] = x.astype(bf16)
            total = jnp.sum(x, axis=0, keepdims=True)
            square = jnp.sum(x * x, axis=0, keepdims=True)
            for stat, line in enumerate((total, square)):
                for tile in range(chunk // LANES):
                    line_row = stat * out_tiles + start // LANES + tile
                    sel_sums_ref[line_row * owners + owner] = line[:, tile * LANES:(tile + 1) * LANES]

    with jax.named_scope("sel_send"):
        each_device(lambda other, where: send(sel_sums_ref.at[other], sel_got.at[me], 1, where))

        def move(k, carry):
            owner = lax.rem(z + k, owners)
            send(dense_ref.at[owner], moved_ref.at[z], 2, {"gx": gx, "gy": gy, "gz": owner})
            return carry

        lax.fori_loop(1, owners, move, 0)
        sel_got[me] = sel_sums_ref[me]
        moved_ref[z] = dense_ref[z]

    with jax.named_scope("wait_rs"):
        finish(recv_sem.at[0], got, n - 1)
    with jax.named_scope("reduce"):
        parts = got[...].astype(f32)
        means = parts[:, :rows]
        mean = jnp.sum(means, axis=0) * (1.0 / n)
        away = means - mean[None]
        variance = jnp.sum(parts[:, rows:] + (away * away) * float(local), axis=0) * (1.0 / cells)
        mine[...] = jnp.concatenate([mean, variance], axis=0).astype(bf16)
    with jax.named_scope("gather_send"):
        each_team(lambda where: send(mine, stats_ref.at[r], 3, where))
    with jax.named_scope("wait_selrs"):
        finish(recv_sem.at[1], sel_got, n - 1)
    with jax.named_scope("selreduce"):
        sel_mine[...] = jnp.sum(sel_got[...], axis=0)
        each_team(lambda where: send(sel_mine, sel_stats_ref.at[r], 4, where))
        stats_ref[r] = mine[...]
        sel_stats_ref[r] = sel_mine[...]
    with jax.named_scope("wait_moved"):
        finish(recv_sem.at[2], moved_ref, owners - 1)
        finish(send_sem.at[0], got, n - 1)
        finish(send_sem.at[1], sel_got, n - 1)
        finish(send_sem.at[2], moved_ref, owners - 1)
    with jax.named_scope("wait_stats"):
        finish(recv_sem.at[3], stats_ref, teams - 1)
    with jax.named_scope("genes"):
        wide[...] = stats_ref[...].astype(f32).reshape(wide.shape)
        lines = rows * LANES // BLOCK * 2
        for stat in range(2):
            for row in range(rows):
                line = wide[pl.ds(stat * rows + row, teams, stride=2 * rows), :]
                turned[row * LANES:(row + 1) * LANES, :] = jnp.transpose(line)
            parts = [turned[pl.ds(k, lines, stride=8), :] for k in range(8)]
            gene_ref[:, stat, :] = jnp.concatenate(parts, axis=1)
    with jax.named_scope("wait_sel"):
        finish(recv_sem.at[4], sel_stats_ref, teams - 1)
    with jax.named_scope("pca"):
        for tile in range(out_tiles):
            mean = sel_stats_ref[tile] * (1.0 / cells)
            variance = sel_stats_ref[out_tiles + tile] * (1.0 / cells) - mean * mean
            scale = 1.0 / jnp.sqrt(jnp.maximum(variance, var_floor))
            cols = slice(tile * LANES, (tile + 1) * LANES)
            for owner in range(owners):
                x = moved_ref[owner, :, cols].astype(f32)
                y = jnp.clip((x - mean) * scale, -clip_value, clip_value)
                pca_ref[owner * local:(owner + 1) * local, cols] = y.astype(bf16)
    with jax.named_scope("wait_sends"):
        finish(send_sem.at[3], stats_ref, teams - 1)
        finish(send_sem.at[4], sel_stats_ref, teams - 1)


def per_device(sizes, columns, counts, nnz_count, selected):
    f32, bf16, i32 = jnp.float32, jnp.bfloat16, jnp.int32
    nx, ny, owners = sizes
    teams = nx * ny
    n = teams * owners
    local, slots = columns.shape
    rows = HIGHS // owners
    share = selected.shape[0] // owners
    assert teams == BLOCK and rows * owners == HIGHS and rows <= 8 and 2 * share // LANES <= teams
    assert local % GROUP == 0
    hbm = pl.BlockSpec(memory_space=pltpu.HBM)
    vmem = pl.BlockSpec(memory_space=pltpu.VMEM)
    lines = GENES // owners // LANES
    slot_rows = local * slots // LANES + 16
    far_rows = HIGHS * local
    arrays = (columns, counts, nnz_count.reshape(1, local), selected.reshape(1, -1))
    gene_stats, pca_input = pl.pallas_call(
        functools.partial(fused_kernel, sizes, local * n),
        name="moments_and_selection",
        out_shape=(pltpu.VMEM((lines, 2, LANES), f32), pltpu.VMEM((owners * local, share), bf16)),
        in_specs=[hbm] * 4,
        out_specs=(vmem,) * 2,
        scratch_shapes=[
            pltpu.VMEM((local, slots), i32),
            pltpu.VMEM((local, slots), i32),
            pltpu.VMEM((1, local), i32),
            pltpu.VMEM((1, owners * share), i32),
        ]
        + [pltpu.VMEM((slot_rows, LANES), f32)] * 4
        + [pltpu.VMEM((local, HIGHS, LANES), f32)] * 3
        + [pltpu.VMEM((far_rows, LANES), f32)] * 2
        + [pltpu.VMEM((BLOCK, HIGHS, LANES), f32)] * 2
        + [
            pltpu.VMEM((far_rows, 2 * LANES), bf16),
            pltpu.VMEM((n, 2 * rows, LANES), bf16),
            pltpu.VMEM((n, 1, LANES), f32),
            pltpu.VMEM((owners, local, share), bf16),
            pltpu.VMEM((n, 2 * rows, LANES), bf16),
            pltpu.VMEM((n, 1, LANES), f32),
            pltpu.VMEM((2 * rows, LANES), bf16),
            pltpu.VMEM((1, LANES), f32),
            pltpu.VMEM((teams, 2 * rows, LANES), bf16),
            pltpu.VMEM((teams, 1, LANES), f32),
            pltpu.VMEM((owners, local, share), bf16),
            pltpu.VMEM((teams * 2 * rows, LANES), f32),
            pltpu.VMEM((rows * LANES, teams), f32),
            pltpu.SemaphoreType.DMA((2 + 2 * (local // GROUP),)),
            pltpu.SemaphoreType.DMA((5,)),
            pltpu.SemaphoreType.DMA((5,)),
        ],
        compiler_params=pltpu.CompilerParams(
            collective_id=0, has_side_effects=True, vmem_limit_bytes=32 * 1024 * 1024
        ),
    )(*(pltpu.with_memory_space_constraint(array, pltpu.HBM) for array in arrays))
    return (gene_stats.transpose(1, 0, 2).reshape(2, -1), pca_input)


def solution(mesh):
    sizes = tuple(mesh.shape[axis] for axis in ("gx", "gy", "gz"))
    return jax.shard_map(
        functools.partial(per_device, sizes),
        mesh=mesh,
        in_specs=(
            P(("gx", "gy", "gz"), None),
            P(("gx", "gy", "gz"), None),
            P(("gx", "gy", "gz")),
            P(),
        ),
        out_specs=(P(None, "gz"), P(("gx", "gy"), "gz")),
        check_vma=False,
    )
```

time: 23.6 us -> 21.1 us (0.89)
  Pallas kernels: 22.8 us -> 19 us
  local copies, waits for them, and re-layouts: 0 us -> 1.31 us
    pallas_call x2 -> x1, Pallas kernels: 22.8 us -> 19 us  [per_device(): pl.pallas_call(functools.partial(fused_kernel, sizes, local * n), name='m...]
    unnamed x0 -> x2, local copies, waits for them, and re-layouts: none -> 1.31 us
where the time goes in v1:
time: 21.1 us; the launch traced here: 20.9 us
  Pallas kernels  19 us (90%)
  local copies, waits for them, and re-layouts  1.31 us (6%)
  between operations  0.64 us (3%)
    pallas_call x1, Pallas kernels, per_device(): pl.pallas_call(functools.partial(fused_kernel, sizes, local * n), name='m...  19 us
    unnamed x2, local copies, waits for them, and re-layouts  1.31 us

profile of v1, /device:TPU:0, one launch (start us, length us, event | category | flops | bytes accessed | tf_op | source)
XLA Modules:
  0.0 20.9 jit_solution(8990359431522857885)
XLA Ops:
  0.6 19.0 %moments_and_selection.1 = (f32[128,2,128]{2,1,0:T(2,128)S(1)}, bf16[64,1024]{1,0:T(8,128)(2,1)S(1)}) custom-call(s32[32,2048]{1,0:T(8,128)} %columns_hbm.1, s32[32,2048]{1,0:T(8,128)} %counts_hbm.1, s32[1,32]{1,0:T(1,128)} %bitcast.7, s32[1,2048]{1,0:T(1,128)} %bitcast.6), custom_call_target="tpu_custom_call" | custom-call | tf_op jit(solution)/shard_map/moments_and_selection/pallas_call | solution.py:320
  19.6 0.7 %copy.8 = f32[2,16384]{1,0:T(2,128)} copy(f32[2,16384]{1,0:T(2,128)S(1)} %bitcast.5) | data formatting | bytes 262144
  20.3 0.7 %copy.9 = bf16[64,1024]{1,0:T(8,128)(2,1)} copy(bf16[64,1024]{1,0:T(8,128)(2,1)S(1)} %get-tuple-element.7) | data formatting | bytes 262144

commit v2 on v1

--- a/solution.py
+++ b/solution.py
@@ -12,6 +12,9 @@
 LANES = 128
 GROUP = 8
 HIGHS = GENES // (BLOCK * LANES)
+WIDTH = 8
+BASE = 60
+QUARTERS = 4
 
 target_sum = 10000.0
 var_floor = 0.01
@@ -30,11 +33,11 @@
 
 
 def fused_kernel(
-    sizes, cells, columns_hbm, counts_hbm, nnz_hbm, selected_hbm, gene_ref, pca_ref,
-    columns_ref, counts_ref, nnz_ref, selected_ref, value_rows, high_rows, low_rows, offset_rows,
-    near_values, near_squares, near_offsets, far_values, far_offsets, acc_values, acc_squares, table,
-    sums_ref, sel_sums_ref, dense_ref, got, sel_got, mine, sel_mine, stats_ref, sel_stats_ref, moved_ref,
-    wide, turned, load_sem, send_sem, recv_sem,
+    sizes, cells, columns_hbm, counts_hbm, nnz_hbm, selected_hbm, stats_ref, sel_stats_ref, moved_ref,
+    columns_ref, counts_ref, nnz_ref, selected_ref, code_rows, high_rows, low_rows,
+    near_values, near_squares, near_offsets, far_codes, acc_values, acc_squares, table,
+    mean_rows, spare_rows, sums_ref, sel_sums_ref, dense_ref, got, sel_got, mine, sel_mine, turned,
+    load_sem, send_sem, recv_sem,
 ):
     nx, ny, owners = sizes
     teams = nx * ny
@@ -46,7 +49,10 @@
     local, slots = columns_ref.shape
     groups = local // GROUP
     tiles = slots // LANES
+    span_blocks = GENES // (BLOCK * n)
     rows = HIGHS // owners
+    halves = LANES // span_blocks
+    lines = 2 * span_blocks // (LANES // BLOCK)
 
     loads = [pltpu.make_async_copy(nnz_hbm, nnz_ref, load_sem.at[0])]
     for g in range(groups):
@@ -114,24 +120,27 @@
     lane = lax.broadcasted_iota(jnp.int32, (GROUP, local), 1)
     slot = lax.broadcasted_iota(jnp.int32, (GROUP, slots), 1)
 
+    def wait_group(g):
+        loads[1 + 2 * g].wait()
+        loads[2 + 2 * g].wait()
+
     def prepare(g):
-        loads[1 + 2 * g].wait()
         span = slice(g * GROUP, (g + 1) * GROUP)
         live_count = jnp.sum(jnp.where(sub + g * GROUP == lane, nnz_ref[...], 0), axis=1, keepdims=True)
         live = slot < live_count
         raw = jnp.where(live, counts_ref[span, :].astype(f32), 0.0)
         library = jnp.sum(raw, axis=1, keepdims=True)
         value = jnp.log(1.0 + raw * (target_sum / library))
-        loads[2 + 2 * g].wait()
         genes = columns_ref[span, :]
-        upper = (lax.shift_right_logical(genes, 10) & 1) * HIGHS
-        high = (lax.shift_right_logical(genes, 11) + upper).astype(f32)
-        low = (lax.shift_right_logical(genes, 4) & (LANES // 2 - 1)).astype(f32)
-        offset = jnp.where(live, genes & (BLOCK - 1), 0).astype(f32)
+        shift = ((genes & (BLOCK - 1)) * WIDTH - BASE).astype(f32)
+        code = value * jnp.exp2(shift)
+        quarter = lax.shift_right_logical(genes, 9) & (QUARTERS - 1)
+        high = (lax.shift_right_logical(genes, 11) + quarter * HIGHS).astype(f32)
+        low = (lax.shift_right_logical(genes, 4) & (LANES // QUARTERS - 1)).astype(f32)
         for tile in range(tiles):
             at = (g * tiles + tile) * GROUP
             cols = slice(tile * LANES, (tile + 1) * LANES)
-            for ref, line in ((value_rows, value), (high_rows, high), (low_rows, low), (offset_rows, offset)):
+            for ref, line in ((code_rows, code), (high_rows, high), (low_rows, low)):
                 ref[at:at + GROUP, :] = line[:, cols]
 
     def spread(ref, g, j):
@@ -143,23 +152,20 @@
     def place(g, j):
         c = g * GROUP + j
         zero, one = bf16(0.0), bf16(1.0)
-        high = spread(high_rows, g, j)
-        hits = [high == ids + bf16(HIGHS * k) for k in range(2)]
-        value, offset = spread(value_rows, g, j), spread(offset_rows, g, j)
+        high, code, low = spread(high_rows, g, j), spread(code_rows, g, j), spread(low_rows, g, j)
         left = jnp.concatenate(
-            [jnp.where(hit, line, zero) for line in (value, offset) for hit in hits], axis=0
+            [jnp.where(high == ids + bf16(HIGHS * k), code, zero) for k in range(QUARTERS)], axis=0
         )
-        low = spread(low_rows, g, j)
         right = jnp.concatenate(
-            [jnp.where(low == ids + bf16(16 * k), one, zero) for k in range(LANES // 32)], axis=0
+            [jnp.where(low == ids + bf16(16 * k), one, zero) for k in range(LANES // (16 * QUARTERS))], axis=0
         )
         placed = lax.dot_general(left, right, (((1,), (1,)), ((), ())), preferred_element_type=f32)
-        quarters = [placed[HIGHS * k:HIGHS * (k + 1)] for k in range(4)]
-        v = jnp.concatenate(quarters[:2], axis=1)
-        o = jnp.concatenate(quarters[2:], axis=1)
-        near_values[c], near_squares[c], near_offsets[c] = v, v * v, o
-        far_values[pl.ds(c, HIGHS, stride=local), :] = v
-        far_offsets[pl.ds(c, HIGHS, stride=local), :] = o
+        code = jnp.concatenate([placed[HIGHS * k:HIGHS * (k + 1)] for k in range(QUARTERS)], axis=1)
+        far_codes[pl.ds(c, HIGHS, stride=local), :] = code
+        power = jnp.log2(jnp.maximum(code, 2.0 ** (-BASE - WIDTH)))
+        offset = jnp.floor((power + (BASE + 0.5 * WIDTH)) * (1.0 / WIDTH))
+        value = code * jnp.exp2(BASE - WIDTH * offset)
+        near_values[c], near_squares[c], near_offsets[c] = value, value * value, offset
 
     def gather_sums(g, ks):
         total = [jnp.zeros((HIGHS, LANES), f32) if g == 0 else acc_values[k] for k in ks]
@@ -176,24 +182,36 @@
                 acc_values[k], acc_squares[k] = total[i], square[i]
                 continue
             near = total[i] * (1.0 / local)
-            spare = square[i] - total[i] * near
-            for owner in range(owners):
-                part = slice(owner * rows, (owner + 1) * rows)
-                sums_ref[k * owners + owner] = jnp.concatenate([near[part], spare[part]], axis=0).astype(bf16)
+            mean_rows[pl.ds(k, HIGHS, stride=BLOCK), :] = near
+            spare_rows[pl.ds(k, HIGHS, stride=BLOCK), :] = square[i] - total[i] * near
 
     per_cell = BLOCK // GROUP
     loads[0].wait()
+    wait_group(0)
+    with jax.named_scope("prep"):
+        prepare(0)
+    for g in range(1, groups):
+        wait_group(g)
     for g in range(groups):
-        with jax.named_scope("prep"):
-            prepare(g)
         with jax.named_scope("place"):
             for j in range(GROUP):
                 place(g, j)
                 if g:
                     gather_sums(g - 1, range(j * per_cell, (j + 1) * per_cell))
+                if j == 0 and g < groups - 1:
+                    prepare(g + 1)
     with jax.named_scope("tail"):
         for j in range(GROUP):
             gather_sums(groups - 1, range(j * per_cell, (j + 1) * per_cell))
+        for high in range(HIGHS):
+            near, spare = (ref[high * BLOCK:(high + 1) * BLOCK, :] for ref in (mean_rows, spare_rows))
+            for half in range(halves):
+                cols = slice(half * span_blocks, (half + 1) * span_blocks)
+                pair = jnp.concatenate([near[:, cols], spare[:, cols]], axis=1)
+                if 2 * span_blocks < LANES:
+                    pair = jnp.concatenate([pair, jnp.zeros((BLOCK, LANES - 2 * span_blocks), f32)], axis=1)
+                team = (high % rows) * halves + half
+                sums_ref[team * owners + high // rows] = pair.astype(bf16)
 
     with jax.named_scope("barrier_wait"):
         pl.semaphore_wait(barrier, n - 1)
@@ -207,11 +225,9 @@
         chunk = min(256, share)
         pairs = HIGHS // 2
         for pair in range(pairs):
-            for part, ref in enumerate((far_values, far_offsets)):
-                at = 2 * pair * local
-                line = jnp.concatenate([ref[at:at + local, :], ref[at + local:at + 2 * local, :]], axis=1)
-                at = (2 * pair + part) * local
-                table[at:at + local, :] = line.astype(bf16)
+            at = 2 * pair * local
+            line = jnp.concatenate([far_codes[at:at + local, :], far_codes[at + local:at + 2 * local, :]], axis=1)
+            table[pair * local:(pair + 1) * local, :] = line.astype(bf16)
         sel_sums_ref[...] = jnp.zeros_like(sel_sums_ref)
         chunk_ids = lax.broadcasted_iota(jnp.int32, (16, chunk), 0).astype(f32).astype(bf16)
         loads[1 + 2 * groups].wait()
@@ -223,12 +239,12 @@
                 [jnp.where(inside == chunk_ids + bf16(16 * k), bf16(1.0), bf16(0.0)) for k in range(16)], axis=0
             )
             found = jnp.dot(table[...], one_hot, preferred_element_type=f32)
-            which = jnp.broadcast_to(lax.shift_right_logical(picked, 12), (2 * local, chunk))
-            mix = found[:2 * local]
+            which = jnp.broadcast_to(lax.shift_right_logical(picked, 12), (local, chunk))
+            mix = found[:local]
             for pair in range(1, pairs):
-                mix = jnp.where(which == pair, found[2 * local * pair:2 * local * (pair + 1)], mix)
-            wanted = (picked & (BLOCK - 1)).astype(f32)
-            x = jnp.where(mix[local:] == wanted, mix[:local], 0.0)
+                mix = jnp.where(which == pair, found[local * pair:local * (pair + 1)], mix)
+            value = mix * jnp.exp2((BASE - (picked & (BLOCK - 1)) * WIDTH).astype(f32))
+            x = jnp.where((value > 2.0 ** -4.5) & (value < 2.0 ** 3.5), value, 0.0)
             owner, start = first // share, first % share
             dense_ref[owner, :, start:start + chunk] = x.astype(bf16)
             total = jnp.sum(x, axis=0, keepdims=True)
@@ -254,11 +270,15 @@
         finish(recv_sem.at[0], got, n - 1)
     with jax.named_scope("reduce"):
         parts = got[...].astype(f32)
-        means = parts[:, :rows]
-        mean = jnp.sum(means, axis=0) * (1.0 / n)
-        away = means - mean[None]
-        variance = jnp.sum(parts[:, rows:] + (away * away) * float(local), axis=0) * (1.0 / cells)
-        mine[...] = jnp.concatenate([mean, variance], axis=0).astype(bf16)
+        total = jnp.sum(parts, axis=0)
+        mean = total * (1.0 / n)
+        away = parts - mean[None]
+        away = pltpu.roll(jnp.sum(away * away, axis=0), span_blocks, 1)
+        variance = (total + away * float(local)) * (1.0 / cells)
+        first_half = lax.broadcasted_iota(jnp.int32, (BLOCK, LANES), 1) < span_blocks
+        turned[...] = jnp.transpose(jnp.where(first_half, mean, variance))
+        pieces = [turned[pl.ds(k, lines, stride=LANES // BLOCK), :] for k in range(LANES // BLOCK)]
+        mine[...] = jnp.concatenate(pieces, axis=1).astype(bf16)
     with jax.named_scope("gather_send"):
         each_team(lambda where: send(mine, stats_ref.at[r], 3, where))
     with jax.named_scope("wait_selrs"):
@@ -275,30 +295,37 @@
         finish(send_sem.at[2], moved_ref, owners - 1)
     with jax.named_scope("wait_stats"):
         finish(recv_sem.at[3], stats_ref, teams - 1)
-    with jax.named_scope("genes"):
-        wide[...] = stats_ref[...].astype(f32).reshape(wide.shape)
-        lines = rows * LANES // BLOCK * 2
-        for stat in range(2):
-            for row in range(rows):
-                line = wide[pl.ds(stat * rows + row, teams, stride=2 * rows), :]
-                turned[row * LANES:(row + 1) * LANES, :] = jnp.transpose(line)
-            parts = [turned[pl.ds(k, lines, stride=8), :] for k in range(8)]
-            gene_ref[:, stat, :] = jnp.concatenate(parts, axis=1)
     with jax.named_scope("wait_sel"):
         finish(recv_sem.at[4], sel_stats_ref, teams - 1)
-    with jax.named_scope("pca"):
-        for tile in range(out_tiles):
-            mean = sel_stats_ref[tile] * (1.0 / cells)
-            variance = sel_stats_ref[out_tiles + tile] * (1.0 / cells) - mean * mean
-            scale = 1.0 / jnp.sqrt(jnp.maximum(variance, var_floor))
-            cols = slice(tile * LANES, (tile + 1) * LANES)
-            for owner in range(owners):
-                x = moved_ref[owner, :, cols].astype(f32)
-                y = jnp.clip((x - mean) * scale, -clip_value, clip_value)
-                pca_ref[owner * local:(owner + 1) * local, cols] = y.astype(bf16)
-    with jax.named_scope("wait_sends"):
         finish(send_sem.at[3], stats_ref, teams - 1)
         finish(send_sem.at[4], sel_stats_ref, teams - 1)
+
+
+def final_kernel(cells, stats_ref, sel_stats_ref, moved_ref, gene_hbm, pca_hbm, gene_ref, pca_ref, sem):
+    f32, bf16 = jnp.float32, jnp.bfloat16
+    teams, double, lanes = stats_ref.shape
+    lines = double // 2
+    stats = stats_ref[...].astype(f32)
+    for team in range(teams):
+        for stat in range(2):
+            gene_ref[team * lines:(team + 1) * lines, stat, :] = stats[team, stat * lines:(stat + 1) * lines]
+    gene_copy = pltpu.make_async_copy(gene_ref, gene_hbm, sem.at[0])
+    gene_copy.start()
+    owners, local, share = moved_ref.shape
+    tiles = share // lanes
+    for tile in range(tiles):
+        mean = sel_stats_ref[tile] * (1.0 / cells)
+        variance = sel_stats_ref[tiles + tile] * (1.0 / cells) - mean * mean
+        scale = 1.0 / jnp.sqrt(jnp.maximum(variance, var_floor))
+        cols = slice(tile * lanes, (tile + 1) * lanes)
+        for owner in range(owners):
+            x = moved_ref[owner, :, cols].astype(f32)
+            y = jnp.clip((x - mean) * scale, -clip_value, clip_value)
+            pca_ref[owner * local:(owner + 1) * local, cols] = y.astype(bf16)
+    pca_copy = pltpu.make_async_copy(pca_ref, pca_hbm, sem.at[1])
+    pca_copy.start()
+    gene_copy.wait()
+    pca_copy.wait()
 
 
 def per_device(sizes, columns, counts, nnz_count, selected):
@@ -309,44 +336,46 @@
     local, slots = columns.shape
     rows = HIGHS // owners
     share = selected.shape[0] // owners
-    assert teams == BLOCK and rows * owners == HIGHS and rows <= 8 and 2 * share // LANES <= teams
-    assert local % GROUP == 0
+    span_blocks = GENES // (BLOCK * n)
+    double = 2 * span_blocks // (LANES // BLOCK)
+    assert rows * owners == HIGHS and span_blocks * n * BLOCK == GENES and 2 * span_blocks <= LANES
+    assert double % 2 == 0 and 2 * share // LANES <= teams and local % GROUP == 0
     hbm = pl.BlockSpec(memory_space=pltpu.HBM)
     vmem = pl.BlockSpec(memory_space=pltpu.VMEM)
-    lines = GENES // owners // LANES
     slot_rows = local * slots // LANES + 16
     far_rows = HIGHS * local
     arrays = (columns, counts, nnz_count.reshape(1, local), selected.reshape(1, -1))
-    gene_stats, pca_input = pl.pallas_call(
+    kept = pl.pallas_call(
         functools.partial(fused_kernel, sizes, local * n),
         name="moments_and_selection",
-        out_shape=(pltpu.VMEM((lines, 2, LANES), f32), pltpu.VMEM((owners * local, share), bf16)),
+        out_shape=(
+            pltpu.VMEM((teams, double, LANES), bf16),
+            pltpu.VMEM((teams, 1, LANES), f32),
+            pltpu.VMEM((owners, local, share), bf16),
+        ),
         in_specs=[hbm] * 4,
-        out_specs=(vmem,) * 2,
+        out_specs=(vmem,) * 3,
         scratch_shapes=[
             pltpu.VMEM((local, slots), i32),
             pltpu.VMEM((local, slots), i32),
             pltpu.VMEM((1, local), i32),
             pltpu.VMEM((1, owners * share), i32),
         ]
-        + [pltpu.VMEM((slot_rows, LANES), f32)] * 4
+        + [pltpu.VMEM((slot_rows, LANES), f32)] * 3
         + [pltpu.VMEM((local, HIGHS, LANES), f32)] * 3
-        + [pltpu.VMEM((far_rows, LANES), f32)] * 2
+        + [pltpu.VMEM((far_rows, LANES), f32)]
         + [pltpu.VMEM((BLOCK, HIGHS, LANES), f32)] * 2
+        + [pltpu.VMEM((far_rows // 2, 2 * LANES), bf16)]
+        + [pltpu.VMEM((HIGHS * BLOCK, LANES), f32)] * 2
         + [
-            pltpu.VMEM((far_rows, 2 * LANES), bf16),
-            pltpu.VMEM((n, 2 * rows, LANES), bf16),
+            pltpu.VMEM((n, BLOCK, LANES), bf16),
             pltpu.VMEM((n, 1, LANES), f32),
             pltpu.VMEM((owners, local, share), bf16),
-            pltpu.VMEM((n, 2 * rows, LANES), bf16),
+            pltpu.VMEM((n, BLOCK, LANES), bf16),
             pltpu.VMEM((n, 1, LANES), f32),
-            pltpu.VMEM((2 * rows, LANES), bf16),
+            pltpu.VMEM((double, LANES), bf16),
             pltpu.VMEM((1, LANES), f32),
-            pltpu.VMEM((teams, 2 * rows, LANES), bf16),
-            pltpu.VMEM((teams, 1, LANES), f32),
-            pltpu.VMEM((owners, local, share), bf16),
-            pltpu.VMEM((teams * 2 * rows, LANES), f32),
-            pltpu.VMEM((rows * LANES, teams), f32),
+            pltpu.VMEM((LANES, BLOCK), f32),
             pltpu.SemaphoreType.DMA((2 + 2 * (local // GROUP),)),
             pltpu.SemaphoreType.DMA((5,)),
             pltpu.SemaphoreType.DMA((5,)),
@@ -355,6 +384,20 @@
             collective_id=0, has_side_effects=True, vmem_limit_bytes=32 * 1024 * 1024
         ),
     )(*(pltpu.with_memory_space_constraint(array, pltpu.HBM) for array in arrays))
+    out_lines = GENES // owners // LANES
+    gene_stats, pca_input = pl.pallas_call(
+        functools.partial(final_kernel, local * n),
+        name="standardize",
+        out_shape=(pltpu.HBM((out_lines, 2, LANES), f32), pltpu.HBM((owners * local, share), bf16)),
+        in_specs=[vmem] * 3,
+        out_specs=(hbm,) * 2,
+        scratch_shapes=[
+            pltpu.VMEM((out_lines, 2, LANES), f32),
+            pltpu.VMEM((owners * local, share), bf16),
+            pltpu.SemaphoreType.DMA((2,)),
+        ],
+        compiler_params=pltpu.CompilerParams(vmem_limit_bytes=16 * 1024 * 1024),
+    )(*(pltpu.with_memory_space_constraint(array, pltpu.VMEM) for array in kept))
     return (gene_stats.transpose(1, 0, 2).reshape(2, -1), pca_input)
 
 

time: 21.1 us -> 19.4 us (0.919)
  local copies, waits for them, and re-layouts: 1.31 us -> 0 us
  Pallas kernels: 19 us -> 18.5 us
    unnamed x2 -> x0, local copies, waits for them, and re-layouts: 1.31 us -> none
    pallas_call x1, Pallas kernels: 19 us -> 17.7 us  [per_device(): pl.pallas_call(functools.partial(fused_kernel, sizes, local * n), name='m...]
    pallas_call x0 -> x1, Pallas kernels: none -> 0.81 us  [per_device(): pl.pallas_call(functools.partial(final_kernel, local * n), name='standard...]
where the time goes in v2:
time: 19.4 us; the launch traced here: 19.2 us
  Pallas kernels  18.5 us (95%)
  between operations  0.64 us (3%)
    pallas_call x1, Pallas kernels, per_device(): pl.pallas_call(functools.partial(fused_kernel, sizes, local * n), name='m...  17.7 us
    pallas_call x1, Pallas kernels, per_device(): pl.pallas_call(functools.partial(final_kernel, local * n), name='standard...  0.81 us

profile of v2, /device:TPU:0, one launch (start us, length us, event | category | flops | bytes accessed | tf_op | source)
XLA Modules:
  0.0 19.2 jit_solution(18257850321477906891)
XLA Ops:
  0.6 17.7 %moments_and_selection.1 = (bf16[16,16,128]{2,1,0:T(8,128)(2,1)S(1)}, f32[16,1,128]{2,1,0:T(1,128)S(1)}, bf16[2,32,1024]{2,1,0:T(8,128)(2,1)S(1)}) custom-call(s32[32,2048]{1,0:T(8,128)} %columns_hbm.1, s32[32,2048]{1,0:T(8,128)} %counts_hbm.1, s32[1,32]{1,0:T(1,128)} %bitcast.6, s32[1,2048]{1,0:T(1,128)} %bitcast.5), custom_call_target="tpu_custom_call" | custom-call | tf_op jit(solution)/shard_map/moments_and_selection/pallas_call | solution.py:348
  18.4 0.8 %standardize.1 = (f32[128,2,128]{2,1,0:T(2,128)}, bf16[64,1024]{1,0:T(8,128)(2,1)}) custom-call(bf16[16,16,128]{2,1,0:T(8,128)(2,1)S(1)} %get-tuple-element.7.stats_ref, f32[16,1,128]{2,1,0:T(1,128)S(1)} %get-tuple-element.8.sel_stats_ref, bf16[2,32,1024]{2,1,0:T(8,128)(2,1)S(1)} %get-tuple-element.9.moved_ref), custom_call_target="tpu_custom_call" | custom-call | tf_op jit(solution)/shard_map/standardize/pallas_call | solution.py:388

commit v3 on v2

v3 whole, which is shorter than its diff:
```python
import functools

import jax
import jax.numpy as jnp
from jax import lax
from jax.experimental import pallas as pl
from jax.experimental.pallas import tpu as pltpu
from jax.sharding import PartitionSpec as P

GENES = 32768
BLOCK = 16
LANES = 128
GROUP = 8
HIGHS = GENES // (BLOCK * LANES)
WIDTH = 8
BASE = 60
PARTS = 3
PART = -(-LANES // PARTS)

target_sum = 10000.0
var_floor = 0.01
clip_value = 10.0

MESH = pl.DeviceIdType.MESH


def flip(value, k, size):
    out, bit = 0, 1
    while bit < size:
        part = lax.rem(lax.div(value, bit), 2)
        out = out + (1 - part if k & bit else part) * bit
        bit *= 2
    return out


def hub_grid(nx, ny, count):
    across = max(1, count // ny)
    along = count // across
    return across, along, nx // across, ny // along


def fused_kernel(
    sizes, cells, columns_hbm, counts_hbm, nnz_hbm, selected_hbm, stats_ref, sel_stats_ref, moved_ref,
    columns_ref, counts_ref, nnz_ref, selected_ref, code_rows, high_rows, low_rows,
    near_values, near_offsets, far_codes, acc_values, acc_squares, table,
    mean_rows, spare_rows, sums_ref, sel_sums_ref, dense_ref, got, sel_got, mine, sel_mine, turned,
    load_sem, send_sem, recv_sem,
):
    nx, ny, owners = sizes
    teams = nx * ny
    n = teams * owners
    gx, gy, z = lax.axis_index("gx"), lax.axis_index("gy"), lax.axis_index("gz")
    r = gx * ny + gy
    me = r * owners + z
    bf16, f32 = jnp.bfloat16, jnp.float32
    local, slots = columns_ref.shape
    groups = local // GROUP
    tiles = slots // LANES
    hubs = HIGHS // owners
    across, along, step_x, step_y = hub_grid(nx, ny, hubs)
    hub_x, hub_y = lax.div(gx, step_x), lax.div(gy, step_y)
    hub = hub_x * along + hub_y
    is_hub = (gx == hub_x * step_x + step_x - 1) & (gy == hub_y * step_y + step_y - 1)
    is_leaf = jnp.logical_not(is_hub)
    lines = 2 * BLOCK

    loads = [pltpu.make_async_copy(nnz_hbm, nnz_ref, load_sem.at[0])]
    for g in range(groups):
        span = pl.ds(g * GROUP, GROUP)
        loads.append(pltpu.make_async_copy(counts_hbm.at[span], counts_ref.at[span], load_sem.at[1 + 2 * g]))
        loads.append(pltpu.make_async_copy(columns_hbm.at[span], columns_ref.at[span], load_sem.at[2 + 2 * g]))
    loads.append(pltpu.make_async_copy(selected_hbm, selected_ref, load_sem.at[1 + 2 * groups]))
    for load in loads:
        load.start()

    xs = [flip(gx, k, nx) for k in range(nx)]
    ys = [flip(gy, k, ny) for k in range(ny)]
    zs = [flip(z, k, owners) for k in range(owners)]
    hub_xs = [flip(hub_x, k, across) for k in range(across)]
    hub_ys = [flip(hub_y, k, along) for k in range(along)]

    def greet(where):
        pl.semaphore_signal(barrier, inc=1, device_id=where, device_id_type=MESH)

    def each_hub(act):
        for ky in reversed(range(along)):
            for kx in reversed(range(across)):
                for kz in reversed(range(owners)):
                    hx, hy = hub_xs[kx], hub_ys[ky]
                    slot = (hx * along + hy) * owners + zs[kz]
                    where = {"gx": hx * step_x + step_x - 1, "gy": hy * step_y + step_y - 1, "gz": zs[kz]}
                    if ky or kx or kz:
                        act(slot, where)
                    else:
                        pl.when(is_leaf)(functools.partial(act, slot, where))

    def each_team(act):
        for ky in reversed(range(ny)):
            for kx in sorted(range(nx), key=lambda k: (k & 1, k), reverse=True):
                if ky or kx:
                    act({"gx": xs[kx], "gy": ys[ky], "gz": z})

    barrier = pltpu.get_barrier_semaphore()
    if n <= 64:
        for ky in reversed(range(ny)):
            for kx in reversed(range(nx)):
                for kz in reversed(range(owners)):
                    if ky or kx or kz:
                        greet({"gx": xs[kx], "gy": ys[ky], "gz": zs[kz]})
    else:
        def greet_step(k, carry):
            other = lax.rem(me + k, n)
            team, owner = lax.div(other, owners), lax.rem(other, owners)
            greet({"gx": lax.div(team, ny), "gy": lax.rem(team, ny), "gz": owner})
            return carry

        lax.fori_loop(1, n, greet_step, 0)

    def send(src, dst, kind, where):
        pltpu.make_async_remote_copy(
            src_ref=src, dst_ref=dst, send_sem=send_sem.at[kind], recv_sem=recv_sem.at[kind],
            device_id=where, device_id_type=MESH,
        ).start()

    def finish(sem, ref, count):
        if count:
            span = ref.at[pl.ds(0, count)]
            pltpu.make_async_copy(span, span, sem).wait()

    ids = lax.broadcasted_iota(jnp.int32, (16, slots), 0).astype(f32).astype(bf16)
    sub = lax.broadcasted_iota(jnp.int32, (GROUP, local), 0)
    lane = lax.broadcasted_iota(jnp.int32, (GROUP, local), 1)
    slot = lax.broadcasted_iota(jnp.int32, (GROUP, slots), 1)

    def wait_group(g):
        loads[1 + 2 * g].wait()
        loads[2 + 2 * g].wait()

    def prepare(g):
        span = slice(g * GROUP, (g + 1) * GROUP)
        live_count = jnp.sum(jnp.where(sub + g * GROUP == lane, nnz_ref[...], 0), axis=1, keepdims=True)
        live = slot < live_count
        raw = jnp.where(live, counts_ref[span, :].astype(f32), 0.0)
        library = jnp.sum(raw, axis=1, keepdims=True)
        value = jnp.log(1.0 + raw * (target_sum / library))
        genes = columns_ref[span, :]
        shift = ((genes & (BLOCK - 1)) * WIDTH - BASE).astype(f32)
        code = value * jnp.exp2(shift)
        high = lax.shift_right_logical(genes, 11)
        low = lax.shift_right_logical(genes, 4) & (LANES - 1)
        for k in range(1, PARTS):
            past = low >= PART
            high = high + jnp.where(past, HIGHS, 0)
            low = low - jnp.where(past, PART, 0)
        high, low = high.astype(f32), low.astype(f32)
        for tile in range(tiles):
            at = (g * tiles + tile) * GROUP
            cols = slice(tile * LANES, (tile + 1) * LANES)
            for ref, line in ((code_rows, code), (high_rows, high), (low_rows, low)):
                ref[at:at + GROUP, :] = line[:, cols]

    def spread(ref, g, j):
        return jnp.concatenate(
            [ref[pl.ds((g * tiles + tile) * GROUP + j, 16, stride=0), :].astype(bf16) for tile in range(tiles)],
            axis=1,
        )

    def place(g, j):
        c = g * GROUP + j
        zero, one = bf16(0.0), bf16(1.0)
        high, code, low = spread(high_rows, g, j), spread(code_rows, g, j), spread(low_rows, g, j)
        left = jnp.concatenate(
            [jnp.where(high == ids + bf16(HIGHS * k), code, zero) for k in range(PARTS)], axis=0
        )
        right = jnp.concatenate(
            [jnp.where(low == ids + bf16(16 * k), one, zero) for k in range(-(-PART // 16))], axis=0
        )
        placed = lax.dot_general(left, right, (((1,), (1,)), ((), ())), preferred_element_type=f32)
        pieces = [
            placed[HIGHS * k:HIGHS * (k + 1), :min(PART, LANES - k * PART)] for k in range(PARTS)
        ]
        code = jnp.concatenate(pieces, axis=1)
        far_codes[pl.ds(c, HIGHS, stride=local), :] = code
        power = jnp.log2(jnp.maximum(code, 2.0 ** (-BASE - WIDTH)))
        offset = jnp.floor((power + (BASE + 0.5 * WIDTH)) * (1.0 / WIDTH))
        value = code * jnp.exp2(BASE - WIDTH * offset)
        near_values[c], near_offsets[c] = value, offset

    def gather_sums(g, ks):
        total = [jnp.zeros((HIGHS, LANES), f32) if g == 0 else acc_values[k] for k in ks]
        square = [jnp.zeros((HIGHS, LANES), f32) if g == 0 else acc_squares[k] for k in ks]
        for j in range(GROUP):
            c = g * GROUP + j
            v, o = near_values[c], near_offsets[c]
            for i, k in enumerate(ks):
                hit = jnp.where(o == float(k), v, 0.0)
                total[i] = total[i] + hit
                square[i] = square[i] + hit * hit
        for i, k in enumerate(ks):
            if g < groups - 1:
                acc_values[k], acc_squares[k] = total[i], square[i]
                continue
            near = total[i] * (1.0 / local)
            mean_rows[pl.ds(k, HIGHS, stride=BLOCK), :] = near
            spare_rows[pl.ds(k, HIGHS, stride=BLOCK), :] = square[i] - total[i] * near

    per_cell = BLOCK // GROUP
    loads[0].wait()
    wait_group(0)
    with jax.named_scope("prep"):
        prepare(0)
    for g in range(1, groups):
        wait_group(g)
    for g in range(groups):
        with jax.named_scope("place"):
            for j in range(GROUP):
                place(g, j)
                if g:
                    gather_sums(g - 1, range(j * per_cell, (j + 1) * per_cell))
                if j == 0 and g < groups - 1:
                    prepare(g + 1)
    with jax.named_scope("tail"):
        for j in range(GROUP):
            gather_sums(groups - 1, range(j * per_cell, (j + 1) * per_cell))
        for high in range(HIGHS):
            for stat, ref in enumerate((mean_rows, spare_rows)):
                line = ref[high * BLOCK:(high + 1) * BLOCK, :].astype(bf16)
                sums_ref[(high % hubs) * owners + high // hubs, stat * BLOCK:(stat + 1) * BLOCK, :] = line

    with jax.named_scope("barrier_wait"):
        pl.semaphore_wait(barrier, n - 1)
    with jax.named_scope("scatter_send"):
        each_hub(lambda slot, where: send(sums_ref.at[slot], got.at[me], 0, where))
    got[me] = sums_ref[hub * owners + z]

    with jax.named_scope("select"):
        share = dense_ref.shape[2]
        out_tiles = share // LANES
        chunk = min(256, share)
        pairs = HIGHS // 2
        for pair in range(pairs):
            at = 2 * pair * local
            line = jnp.concatenate([far_codes[at:at + local, :], far_codes[at + local:at + 2 * local, :]], axis=1)
            table[pair * local:(pair + 1) * local, :] = line.astype(bf16)
        chunk_ids = lax.broadcasted_iota(jnp.int32, (16, chunk), 0).astype(f32).astype(bf16)
        loads[1 + 2 * groups].wait()
        for first in range(0, owners * share, chunk):
            picked = selected_ref[:, first:first + chunk]
            inside = (lax.shift_right_logical(picked, 4) & (2 * LANES - 1)).astype(f32)
            inside = jnp.broadcast_to(inside, (16, chunk)).astype(bf16)
            one_hot = jnp.concatenate(
                [jnp.where(inside == chunk_ids + bf16(16 * k), bf16(1.0), bf16(0.0)) for k in range(16)], axis=0
            )
            found = jnp.dot(table[...], one_hot, preferred_element_type=f32)
            which = jnp.broadcast_to(lax.shift_right_logical(picked, 12), (local, chunk))
            mix = found[:local]
            for pair in range(1, pairs):
                mix = jnp.where(which == pair, found[local * pair:local * (pair + 1)], mix)
            value = mix * jnp.exp2((BASE - (picked & (BLOCK - 1)) * WIDTH).astype(f32))
            x = jnp.where((value > 2.0 ** -4.5) & (value < 2.0 ** 3.5), value, 0.0)
            owner, start = first // share, first % share
            dense_ref[owner, :, start:start + chunk] = x.astype(bf16)
            total = jnp.sum(x, axis=0, keepdims=True)
            square = jnp.sum(x * x, axis=0, keepdims=True)
            pair = jnp.concatenate([total, square], axis=0)
            for tile in range(chunk // LANES):
                at = (start // LANES + tile) * owners + owner
                sel_sums_ref[at] = pair[:, tile * LANES:(tile + 1) * LANES]

    with jax.named_scope("sel_send"):
        each_hub(lambda slot, where: send(sel_sums_ref.at[slot], sel_got.at[me], 1, where))

        def move(k, carry):
            owner = lax.rem(z + k, owners)
            send(dense_ref.at[owner], moved_ref.at[z], 2, {"gx": gx, "gy": gy, "gz": owner})
            return carry

        lax.fori_loop(1, owners, move, 0)
        sel_got[me] = sel_sums_ref[hub * owners + z]
        moved_ref[z] = dense_ref[z]

    @pl.when(is_hub)
    def _():
        with jax.named_scope("wait_rs"):
            finish(recv_sem.at[0], got, n - 1)
        with jax.named_scope("reduce"):
            means = got[:, :BLOCK, :].astype(f32)
            mean = jnp.sum(means, axis=0) * (1.0 / n)
            away = means - mean[None]
            spare = got[:, BLOCK:, :].astype(f32)
            variance = jnp.sum(spare + (away * away) * float(local), axis=0) * (1.0 / cells)
            turned[:LANES, :] = jnp.transpose(mean)
            turned[LANES:, :] = jnp.transpose(variance)
            pieces = [turned[pl.ds(k, lines, stride=LANES // BLOCK), :] for k in range(LANES // BLOCK)]
            mine[...] = jnp.concatenate(pieces, axis=1).astype(bf16)
        with jax.named_scope("gather_send"):
            each_team(lambda where: send(mine, stats_ref.at[hub], 3, where))
        with jax.named_scope("wait_selrs"):
            finish(recv_sem.at[1], sel_got, n - 1)
        with jax.named_scope("selreduce"):
            sel_mine[...] = jnp.sum(sel_got[...], axis=0)
            each_team(lambda where: send(sel_mine, sel_stats_ref.at[hub], 4, where))
            stats_ref[hub] = mine[...]
            sel_stats_ref[hub] = sel_mine[...]

    with jax.named_scope("wait_moved"):
        finish(recv_sem.at[2], moved_ref, owners - 1)
        finish(send_sem.at[2], moved_ref, owners - 1)

    @pl.when(is_hub)
    def _():
        finish(send_sem.at[0], sums_ref, hubs * owners - 1)
        finish(send_sem.at[1], sel_sums_ref, hubs * owners - 1)
        with jax.named_scope("wait_stats"):
            finish(recv_sem.at[3], stats_ref, hubs - 1)
        with jax.named_scope("wait_sel"):
            finish(recv_sem.at[4], sel_stats_ref, hubs - 1)
            for _ in range(teams - 1):
                finish(send_sem.at[3], stats_ref, 1)
                finish(send_sem.at[4], sel_stats_ref, 1)

    @pl.when(is_leaf)
    def _():
        finish(send_sem.at[0], sums_ref, hubs * owners)
        finish(send_sem.at[1], sel_sums_ref, hubs * owners)
        with jax.named_scope("wait_stats"):
            finish(recv_sem.at[3], stats_ref, hubs)
        with jax.named_scope("wait_sel"):
            finish(recv_sem.at[4], sel_stats_ref, hubs)


def final_kernel(cells, stats_ref, sel_stats_ref, moved_ref, gene_hbm, pca_hbm, gene_ref, pca_ref, sem):
    f32, bf16 = jnp.float32, jnp.bfloat16
    hubs, double, lanes = stats_ref.shape
    lines = double // 2
    stats = stats_ref[...].astype(f32)
    for hub in range(hubs):
        for stat in range(2):
            gene_ref[hub * lines:(hub + 1) * lines, stat, :] = stats[hub, stat * lines:(stat + 1) * lines]
    gene_copy = pltpu.make_async_copy(gene_ref, gene_hbm, sem.at[0])
    gene_copy.start()
    owners, local, share = moved_ref.shape
    tiles = share // lanes
    for tile in range(tiles):
        mean = sel_stats_ref[tile, 0:1, :] * (1.0 / cells)
        variance = sel_stats_ref[tile, 1:2, :] * (1.0 / cells) - mean * mean
        scale = 1.0 / jnp.sqrt(jnp.maximum(variance, var_floor))
        cols = slice(tile * lanes, (tile + 1) * lanes)
        for owner in range(owners):
            x = moved_ref[owner, :, cols].astype(f32)
            y = jnp.clip((x - mean) * scale, -clip_value, clip_value)
            pca_ref[owner * local:(owner + 1) * local, cols] = y.astype(bf16)
    pca_copy = pltpu.make_async_copy(pca_ref, pca_hbm, sem.at[1])
    pca_copy.start()
    gene_copy.wait()
    pca_copy.wait()


def per_device(sizes, columns, counts, nnz_count, selected):
    f32, bf16, i32 = jnp.float32, jnp.bfloat16, jnp.int32
    nx, ny, owners = sizes
    teams = nx * ny
    n = teams * owners
    local, slots = columns.shape
    hubs = HIGHS // owners
    across, along, step_x, step_y = hub_grid(nx, ny, hubs)
    share = selected.shape[0] // owners
    assert hubs * owners == HIGHS and across * along == hubs and across * step_x == nx and along * step_y == ny
    assert share == hubs * LANES and local % GROUP == 0
    hbm = pl.BlockSpec(memory_space=pltpu.HBM)
    vmem = pl.BlockSpec(memory_space=pltpu.VMEM)
    slot_rows = local * slots // LANES + 16
    far_rows = HIGHS * local
    arrays = (columns, counts, nnz_count.reshape(1, local), selected.reshape(1, -1))
    kept = pl.pallas_call(
        functools.partial(fused_kernel, sizes, local * n),
        name="moments_and_selection",
        out_shape=(
            pltpu.VMEM((hubs, 2 * BLOCK, LANES), bf16),
            pltpu.VMEM((hubs, 2, LANES), f32),
            pltpu.VMEM((owners, local, share), bf16),
        ),
        in_specs=[hbm] * 4,
        out_specs=(vmem,) * 3,
        scratch_shapes=[
            pltpu.VMEM((local, slots), i32),
            pltpu.VMEM((local, slots), i32),
            pltpu.VMEM((1, local), i32),
            pltpu.VMEM((1, owners * share), i32),
        ]
        + [pltpu.VMEM((slot_rows, LANES), f32)] * 3
        + [pltpu.VMEM((local, HIGHS, LANES), f32)] * 2
        + [pltpu.VMEM((far_rows, LANES), f32)]
        + [pltpu.VMEM((BLOCK, HIGHS, LANES), f32)] * 2
        + [pltpu.VMEM((far_rows // 2, 2 * LANES), bf16)]
        + [pltpu.VMEM((HIGHS * BLOCK, LANES), f32)] * 2
        + [
            pltpu.VMEM((HIGHS, 2 * BLOCK, LANES), bf16),
            pltpu.VMEM((HIGHS, 2, LANES), f32),
            pltpu.VMEM((owners, local, share), bf16),
            pltpu.VMEM((n, 2 * BLOCK, LANES), bf16),
            pltpu.VMEM((n, 2, LANES), f32),
            pltpu.VMEM((2 * BLOCK, LANES), bf16),
            pltpu.VMEM((2, LANES), f32),
            pltpu.VMEM((2 * LANES, BLOCK), f32),
            pltpu.SemaphoreType.DMA((2 + 2 * (local // GROUP),)),
            pltpu.SemaphoreType.DMA((5,)),
            pltpu.SemaphoreType.DMA((5,)),
        ],
        compiler_params=pltpu.CompilerParams(
            collective_id=0, has_side_effects=True, vmem_limit_bytes=32 * 1024 * 1024
        ),
    )(*(pltpu.with_memory_space_constraint(array, pltpu.HBM) for array in arrays))
    out_lines = GENES // owners // LANES
    gene_stats, pca_input = pl.pallas_call(
        functools.partial(final_kernel, local * n),
        name="standardize",
        out_shape=(pltpu.HBM((out_lines, 2, LANES), f32), pltpu.HBM((owners * local, share), bf16)),
        in_specs=[vmem] * 3,
        out_specs=(hbm,) * 2,
        scratch_shapes=[
            pltpu.VMEM((out_lines, 2, LANES), f32),
            pltpu.VMEM((owners * local, share), bf16),
            pltpu.SemaphoreType.DMA((2,)),
        ],
        compiler_params=pltpu.CompilerParams(vmem_limit_bytes=16 * 1024 * 1024),
    )(*(pltpu.with_memory_space_constraint(array, pltpu.VMEM) for array in kept))
    return (gene_stats.transpose(1, 0, 2).reshape(2, -1), pca_input)


def solution(mesh):
    sizes = tuple(mesh.shape[axis] for axis in ("gx", "gy", "gz"))
    return jax.shard_map(
        functools.partial(per_device, sizes),
        mesh=mesh,
        in_specs=(
            P(("gx", "gy", "gz"), None),
            P(("gx", "gy", "gz"), None),
            P(("gx", "gy", "gz")),
            P(),
        ),
        out_specs=(P(None, "gz"), P(("gx", "gy"), "gz")),
        check_vma=False,
    )
```

time: 19.4 us -> 18.6 us (0.959)
  Pallas kernels: 18.5 us -> 17.8 us
    pallas_call x1, Pallas kernels: 17.7 us -> 17 us  [per_device(): pl.pallas_call(functools.partial(fused_kernel, sizes, local * n), name='m...]
where the time goes in v3:
time: 18.6 us; the launch traced here: 18.4 us
  Pallas kernels  17.8 us (96%)
  between operations  0.64 us (3%)
    pallas_call x1, Pallas kernels, per_device(): pl.pallas_call(functools.partial(fused_kernel, sizes, local * n), name='m...  17 us
    pallas_call x1, Pallas kernels, per_device(): pl.pallas_call(functools.partial(final_kernel, local * n), name='standard...  0.81 us

profile of v3, /device:TPU:0, one launch (start us, length us, event | category | flops | bytes accessed | tf_op | source)
XLA Modules:
  0.0 18.4 jit_solution(11229407579104065918)
XLA Ops:
  0.6 17.0 %moments_and_selection.1 = (bf16[8,32,128]{2,1,0:T(8,128)(2,1)S(1)}, f32[8,2,128]{2,1,0:T(2,128)S(1)}, bf16[2,32,1024]{2,1,0:T(8,128)(2,1)S(1)}) custom-call(s32[32,2048]{1,0:T(8,128)} %columns_hbm.1, s32[32,2048]{1,0:T(8,128)} %counts_hbm.1, s32[1,32]{1,0:T(1,128)} %bitcast.6, s32[1,2048]{1,0:T(1,128)} %bitcast.5), custom_call_target="tpu_custom_call" | custom-call | tf_op jit(solution)/shard_map/moments_and_selection/pallas_call | solution.py:375
  17.6 0.8 %standardize.1 = (f32[128,2,128]{2,1,0:T(2,128)}, bf16[64,1024]{1,0:T(8,128)(2,1)}) custom-call(bf16[8,32,128]{2,1,0:T(8,128)(2,1)S(1)} %get-tuple-element.7.stats_ref, f32[8,2,128]{2,1,0:T(2,128)S(1)} %get-tuple-element.8.sel_stats_ref, bf16[2,32,1024]{2,1,0:T(8,128)(2,1)S(1)} %get-tuple-element.9.moved_ref), custom_call_target="tpu_custom_call" | custom-call | tf_op jit(solution)/shard_map/standardize/pallas_call | solution.py:415

commit v4 on v3

--- a/solution.py
+++ b/solution.py
@@ -82,8 +82,8 @@
     def greet(where):
         pl.semaphore_signal(barrier, inc=1, device_id=where, device_id_type=MESH)
 
-    def each_hub(act):
-        for ky in reversed(range(along)):
+    def each_hub(act, kys):
+        for ky in kys:
             for kx in reversed(range(across)):
                 for kz in reversed(range(owners)):
                     hx, hy = hub_xs[kx], hub_ys[ky]
@@ -93,6 +93,9 @@
                         act(slot, where)
                     else:
                         pl.when(is_leaf)(functools.partial(act, slot, where))
+
+    steps = list(reversed(range(along)))
+    far_steps, near_steps = steps[:along // 2], steps[along // 2:]
 
     def each_team(act):
         for ky in reversed(range(ny)):
@@ -230,7 +233,7 @@
     with jax.named_scope("barrier_wait"):
         pl.semaphore_wait(barrier, n - 1)
     with jax.named_scope("scatter_send"):
-        each_hub(lambda slot, where: send(sums_ref.at[slot], got.at[me], 0, where))
+        each_hub(lambda slot, where: send(sums_ref.at[slot], got.at[me], 0, where), far_steps)
     got[me] = sums_ref[hub * owners + z]
 
     with jax.named_scope("select"):
@@ -268,7 +271,8 @@
                 sel_sums_ref[at] = pair[:, tile * LANES:(tile + 1) * LANES]
 
     with jax.named_scope("sel_send"):
-        each_hub(lambda slot, where: send(sel_sums_ref.at[slot], sel_got.at[me], 1, where))
+        each_hub(lambda slot, where: send(sel_sums_ref.at[slot], sel_got.at[me], 1, where), far_steps + near_steps)
+        each_hub(lambda slot, where: send(sums_ref.at[slot], got.at[me], 0, where), near_steps)
 
         def move(k, carry):
             owner = lax.rem(z + k, owners)
@@ -281,6 +285,12 @@
 
     @pl.when(is_hub)
     def _():
+        with jax.named_scope("wait_selrs"):
+            finish(recv_sem.at[1], sel_got, n - 1)
+        with jax.named_scope("selreduce"):
+            sel_mine[...] = jnp.sum(sel_got[...], axis=0)
+            each_team(lambda where: send(sel_mine, sel_stats_ref.at[hub], 4, where))
+            sel_stats_ref[hub] = sel_mine[...]
         with jax.named_scope("wait_rs"):
             finish(recv_sem.at[0], got, n - 1)
         with jax.named_scope("reduce"):
@@ -295,13 +305,7 @@
             mine[...] = jnp.concatenate(pieces, axis=1).astype(bf16)
         with jax.named_scope("gather_send"):
             each_team(lambda where: send(mine, stats_ref.at[hub], 3, where))
-        with jax.named_scope("wait_selrs"):
-            finish(recv_sem.at[1], sel_got, n - 1)
-        with jax.named_scope("selreduce"):
-            sel_mine[...] = jnp.sum(sel_got[...], axis=0)
-            each_team(lambda where: send(sel_mine, sel_stats_ref.at[hub], 4, where))
             stats_ref[hub] = mine[...]
-            sel_stats_ref[hub] = sel_mine[...]
 
     with jax.named_scope("wait_moved"):
         finish(recv_sem.at[2], moved_ref, owners - 1)

time: 18.6 us -> 18 us (0.968)
  Pallas kernels: 17.8 us -> 17.2 us
    pallas_call x1, Pallas kernels: 17 us -> 16.4 us  [per_device(): pl.pallas_call(functools.partial(fused_kernel, sizes, local * n), name='m...]
where the time goes in v4:
time: 18 us; the launch traced here: 17.8 us
  Pallas kernels  17.2 us (96%)
  between operations  0.64 us (4%)
    pallas_call x1, Pallas kernels, per_device(): pl.pallas_call(functools.partial(fused_kernel, sizes, local * n), name='m...  16.4 us
    pallas_call x1, Pallas kernels, per_device(): pl.pallas_call(functools.partial(final_kernel, local * n), name='standard...  0.81 us

profile of v4, /device:TPU:0, one launch (start us, length us, event | category | flops | bytes accessed | tf_op | source)
XLA Modules:
  0.0 17.8 jit_solution(1683944295933131278)
XLA Ops:
  0.6 16.4 %moments_and_selection.1 = (bf16[8,32,128]{2,1,0:T(8,128)(2,1)S(1)}, f32[8,2,128]{2,1,0:T(2,128)S(1)}, bf16[2,32,1024]{2,1,0:T(8,128)(2,1)S(1)}) custom-call(s32[32,2048]{1,0:T(8,128)} %columns_hbm.1, s32[32,2048]{1,0:T(8,128)} %counts_hbm.1, s32[1,32]{1,0:T(1,128)} %bitcast.6, s32[1,2048]{1,0:T(1,128)} %bitcast.5), custom_call_target="tpu_custom_call" | custom-call | tf_op jit(solution)/shard_map/moments_and_selection/pallas_call | solution.py:379
  17.0 0.8 %standardize.1 = (f32[128,2,128]{2,1,0:T(2,128)}, bf16[64,1024]{1,0:T(8,128)(2,1)}) custom-call(bf16[8,32,128]{2,1,0:T(8,128)(2,1)S(1)} %get-tuple-element.7.stats_ref, f32[8,2,128]{2,1,0:T(2,128)S(1)} %get-tuple-element.8.sel_stats_ref, bf16[2,32,1024]{2,1,0:T(8,128)(2,1)S(1)} %get-tuple-element.9.moved_ref), custom_call_target="tpu_custom_call" | custom-call | tf_op jit(solution)/shard_map/standardize/pallas_call | solution.py:419

commit v5 on v4

--- a/solution.py
+++ b/solution.py
@@ -98,10 +98,12 @@
     far_steps, near_steps = steps[:along // 2], steps[along // 2:]
 
     def each_team(act):
-        for ky in reversed(range(ny)):
+        for y in range(ny):
             for kx in sorted(range(nx), key=lambda k: (k & 1, k), reverse=True):
-                if ky or kx:
-                    act({"gx": xs[kx], "gy": ys[ky], "gz": z})
+                if kx:
+                    act({"gx": xs[kx], "gy": y, "gz": z})
+                else:
+                    pl.when(gy != y)(functools.partial(act, {"gx": gx, "gy": y, "gz": z}))
 
     barrier = pltpu.get_barrier_semaphore()
     if n <= 64:
@@ -285,12 +287,6 @@
 
     @pl.when(is_hub)
     def _():
-        with jax.named_scope("wait_selrs"):
-            finish(recv_sem.at[1], sel_got, n - 1)
-        with jax.named_scope("selreduce"):
-            sel_mine[...] = jnp.sum(sel_got[...], axis=0)
-            each_team(lambda where: send(sel_mine, sel_stats_ref.at[hub], 4, where))
-            sel_stats_ref[hub] = sel_mine[...]
         with jax.named_scope("wait_rs"):
             finish(recv_sem.at[0], got, n - 1)
         with jax.named_scope("reduce"):
@@ -303,6 +299,12 @@
             turned[LANES:, :] = jnp.transpose(variance)
             pieces = [turned[pl.ds(k, lines, stride=LANES // BLOCK), :] for k in range(LANES // BLOCK)]
             mine[...] = jnp.concatenate(pieces, axis=1).astype(bf16)
+        with jax.named_scope("wait_selrs"):
+            finish(recv_sem.at[1], sel_got, n - 1)
+        with jax.named_scope("selreduce"):
+            sel_mine[...] = jnp.sum(sel_got[...], axis=0)
+            each_team(lambda where: send(sel_mine, sel_stats_ref.at[hub], 4, where))
+            sel_stats_ref[hub] = sel_mine[...]
         with jax.named_scope("gather_send"):
             each_team(lambda where: send(mine, stats_ref.at[hub], 3, where))
             stats_ref[hub] = mine[...]

time: 18 us -> 17.8 us (0.989)
  Pallas kernels: 17.2 us -> 17 us
where the time goes in v5:
time: 17.8 us; the launch traced here: 17.7 us
  Pallas kernels  17 us (96%)
  between operations  0.64 us (4%)
    pallas_call x1, Pallas kernels, per_device(): pl.pallas_call(functools.partial(fused_kernel, sizes, local * n), name='m...  16.2 us
    pallas_call x1, Pallas kernels, per_device(): pl.pallas_call(functools.partial(final_kernel, local * n), name='standard...  0.81 us

profile of v5, /device:TPU:0, one launch (start us, length us, event | category | flops | bytes accessed | tf_op | source)
XLA Modules:
  0.0 17.7 jit_solution(10332532888824304933)
XLA Ops:
  0.6 16.2 %moments_and_selection.1 = (bf16[8,32,128]{2,1,0:T(8,128)(2,1)S(1)}, f32[8,2,128]{2,1,0:T(2,128)S(1)}, bf16[2,32,1024]{2,1,0:T(8,128)(2,1)S(1)}) custom-call(s32[32,2048]{1,0:T(8,128)} %columns_hbm.1, s32[32,2048]{1,0:T(8,128)} %counts_hbm.1, s32[1,32]{1,0:T(1,128)} %bitcast.6, s32[1,2048]{1,0:T(1,128)} %bitcast.5), custom_call_target="tpu_custom_call" | custom-call | tf_op jit(solution)/shard_map/moments_and_selection/pallas_call | solution.py:381
  16.9 0.8 %standardize.1 = (f32[128,2,128]{2,1,0:T(2,128)}, bf16[64,1024]{1,0:T(8,128)(2,1)}) custom-call(bf16[8,32,128]{2,1,0:T(8,128)(2,1)S(1)} %get-tuple-element.7.stats_ref, f32[8,2,128]{2,1,0:T(2,128)S(1)} %get-tuple-element.8.sel_stats_ref, bf16[2,32,1024]{2,1,0:T(8,128)(2,1)S(1)} %get-tuple-element.9.moved_ref), custom_call_target="tpu_custom_call" | custom-call | tf_op jit(solution)/shard_map/standardize/pallas_call | solution.py:421

commit v6 on v5

--- a/solution.py
+++ b/solution.py
@@ -40,10 +40,10 @@
 
 
 def fused_kernel(
-    sizes, cells, columns_hbm, counts_hbm, nnz_hbm, selected_hbm, stats_ref, sel_stats_ref, moved_ref,
+    sizes, cells, columns_hbm, counts_hbm, nnz_hbm, selected_hbm, stats_ref, pca_ref,
     columns_ref, counts_ref, nnz_ref, selected_ref, code_rows, high_rows, low_rows,
     near_values, near_offsets, far_codes, acc_values, acc_squares, table,
-    mean_rows, spare_rows, sums_ref, sel_sums_ref, dense_ref, got, sel_got, mine, sel_mine, turned,
+    mean_rows, spare_rows, sums_ref, sel_sums_ref, dense_ref, got, sel_got, mine, sel_mine, sel_stats_ref, moved_ref, turned,
     load_sem, send_sem, recv_sem,
 ):
     nx, ny, owners = sizes
@@ -317,49 +317,50 @@
     def _():
         finish(send_sem.at[0], sums_ref, hubs * owners - 1)
         finish(send_sem.at[1], sel_sums_ref, hubs * owners - 1)
-        with jax.named_scope("wait_stats"):
-            finish(recv_sem.at[3], stats_ref, hubs - 1)
-        with jax.named_scope("wait_sel"):
-            finish(recv_sem.at[4], sel_stats_ref, hubs - 1)
-            for _ in range(teams - 1):
-                finish(send_sem.at[3], stats_ref, 1)
-                finish(send_sem.at[4], sel_stats_ref, 1)
+        finish(recv_sem.at[4], sel_stats_ref, hubs - 1)
 
     @pl.when(is_leaf)
     def _():
         finish(send_sem.at[0], sums_ref, hubs * owners)
         finish(send_sem.at[1], sel_sums_ref, hubs * owners)
-        with jax.named_scope("wait_stats"):
-            finish(recv_sem.at[3], stats_ref, hubs)
-        with jax.named_scope("wait_sel"):
-            finish(recv_sem.at[4], sel_stats_ref, hubs)
-
-
-def final_kernel(cells, stats_ref, sel_stats_ref, moved_ref, gene_hbm, pca_hbm, gene_ref, pca_ref, sem):
-    f32, bf16 = jnp.float32, jnp.bfloat16
+        finish(recv_sem.at[4], sel_stats_ref, hubs)
+
+    with jax.named_scope("pca"):
+        for tile in range(out_tiles):
+            mean = sel_stats_ref[tile, 0:1, :] * (1.0 / cells)
+            variance = sel_stats_ref[tile, 1:2, :] * (1.0 / cells) - mean * mean
+            scale = 1.0 / jnp.sqrt(jnp.maximum(variance, var_floor))
+            cols = slice(tile * LANES, (tile + 1) * LANES)
+            for owner in range(owners):
+                x = moved_ref[owner, :, cols].astype(f32)
+                y = jnp.clip((x - mean) * scale, -clip_value, clip_value)
+                pca_ref[owner * local:(owner + 1) * local, cols] = y.astype(bf16)
+
+    @pl.when(is_hub)
+    def _():
+        finish(recv_sem.at[3], stats_ref, hubs - 1)
+        for _ in range(teams - 1):
+            finish(send_sem.at[3], stats_ref, 1)
+            finish(send_sem.at[4], sel_stats_ref, 1)
+
+    @pl.when(is_leaf)
+    def _():
+        finish(recv_sem.at[3], stats_ref, hubs)
+
+
+def final_kernel(stats_ref, pca_ref, gene_hbm, pca_hbm, gene_ref, sem):
+    pca_copy = pltpu.make_async_copy(pca_ref, pca_hbm, sem.at[1])
+    pca_copy.start()
     hubs, double, lanes = stats_ref.shape
     lines = double // 2
-    stats = stats_ref[...].astype(f32)
+    stats = stats_ref[...].astype(jnp.float32)
     for hub in range(hubs):
         for stat in range(2):
             gene_ref[hub * lines:(hub + 1) * lines, stat, :] = stats[hub, stat * lines:(stat + 1) * lines]
     gene_copy = pltpu.make_async_copy(gene_ref, gene_hbm, sem.at[0])
     gene_copy.start()
-    owners, local, share = moved_ref.shape
-    tiles = share // lanes
-    for tile in range(tiles):
-        mean = sel_stats_ref[tile, 0:1, :] * (1.0 / cells)
-        variance = sel_stats_ref[tile, 1:2, :] * (1.0 / cells) - mean * mean
-        scale = 1.0 / jnp.sqrt(jnp.maximum(variance, var_floor))
-        cols = slice(tile * lanes, (tile + 1) * lanes)
-        for owner in range(owners):
-            x = moved_ref[owner, :, cols].astype(f32)
-            y = jnp.clip((x - mean) * scale, -clip_value, clip_value)
-            pca_ref[owner * local:(owner + 1) * local, cols] = y.astype(bf16)
-    pca_copy = pltpu.make_async_copy(pca_ref, pca_hbm, sem.at[1])
-    pca_copy.start()
+    pca_copy.wait()
     gene_copy.wait()
-    pca_copy.wait()
 
 
 def per_device(sizes, columns, counts, nnz_count, selected):
@@ -383,11 +384,10 @@
         name="moments_and_selection",
         out_shape=(
             pltpu.VMEM((hubs, 2 * BLOCK, LANES), bf16),
-            pltpu.VMEM((hubs, 2, LANES), f32),
-            pltpu.VMEM((owners, local, share), bf16),
+            pltpu.VMEM((owners * local, share), bf16),
         ),
         in_specs=[hbm] * 4,
-        out_specs=(vmem,) * 3,
+        out_specs=(vmem,) * 2,
         scratch_shapes=[
             pltpu.VMEM((local, slots), i32),
             pltpu.VMEM((local, slots), i32),
@@ -408,6 +408,8 @@
             pltpu.VMEM((n, 2, LANES), f32),
             pltpu.VMEM((2 * BLOCK, LANES), bf16),
             pltpu.VMEM((2, LANES), f32),
+            pltpu.VMEM((hubs, 2, LANES), f32),
+            pltpu.VMEM((owners, local, share), bf16),
             pltpu.VMEM((2 * LANES, BLOCK), f32),
             pltpu.SemaphoreType.DMA((2 + 2 * (local // GROUP),)),
             pltpu.SemaphoreType.DMA((5,)),
@@ -419,14 +421,13 @@
     )(*(pltpu.with_memory_space_constraint(array, pltpu.HBM) for array in arrays))
     out_lines = GENES // owners // LANES
     gene_stats, pca_input = pl.pallas_call(
-        functools.partial(final_kernel, local * n),
+        final_kernel,
         name="standardize",
         out_shape=(pltpu.HBM((out_lines, 2, LANES), f32), pltpu.HBM((owners * local, share), bf16)),
-        in_specs=[vmem] * 3,
+        in_specs=[vmem] * 2,
         out_specs=(hbm,) * 2,
         scratch_shapes=[
             pltpu.VMEM((out_lines, 2, LANES), f32),
-            pltpu.VMEM((owners * local, share), bf16),
             pltpu.SemaphoreType.DMA((2,)),
         ],
         compiler_params=pltpu.CompilerParams(vmem_limit_bytes=16 * 1024 * 1024),

time: 17.8 us -> 17.8 us (level)
  no operation moved by 1% of the time
where the time goes in v6:
time: 17.8 us; the launch traced here: 17.6 us
  Pallas kernels  17 us (96%)
  between operations  0.64 us (4%)
    pallas_call x1, Pallas kernels, per_device(): pl.pallas_call(functools.partial(fused_kernel, sizes, local * n), name='m...  16.2 us
    pallas_call x1, Pallas kernels, per_device(): pl.pallas_call(final_kernel, name='standardize', out_shape=(pltpu.HBM((ou...  0.75 us

profile of v6, /device:TPU:0, one launch (start us, length us, event | category | flops | bytes accessed | tf_op | source)
XLA Modules:
  0.0 17.6 jit_solution(12208806637640659649)
XLA Ops:
  0.6 16.2 %moments_and_selection.1 = (bf16[8,32,128]{2,1,0:T(8,128)(2,1)S(1)}, bf16[64,1024]{1,0:T(8,128)(2,1)S(1)}) custom-call(s32[32,2048]{1,0:T(8,128)} %columns_hbm.1, s32[32,2048]{1,0:T(8,128)} %counts_hbm.1, s32[1,32]{1,0:T(1,128)} %bitcast.6, s32[1,2048]{1,0:T(1,128)} %bitcast.5), custom_call_target="tpu_custom_call" | custom-call | tf_op jit(solution)/shard_map/moments_and_selection/pallas_call | solution.py:382
  16.9 0.7 %standardize.1 = (f32[128,2,128]{2,1,0:T(2,128)}, bf16[64,1024]{1,0:T(8,128)(2,1)}) custom-call(bf16[8,32,128]{2,1,0:T(8,128)(2,1)S(1)} %get-tuple-element.6.stats_ref, bf16[64,1024]{1,0:T(8,128)(2,1)S(1)} %get-tuple-element.7.pca_ref), custom_call_target="tpu_custom_call" | custom-call | tf_op jit(solution)/shard_map/standardize/pallas_call | solution.py:423
